TPU v7x, 32 devices: a whole 2x2x4 slice. The times are simulated.
32 devices in a mesh: row: 4 (over y, x), col: 8 (over z, core).
Axes of the slice: x: 2, y: 2, z: 4, core: 2. Of those that a mesh axis runs over, the one named last changes fastest.
Arguments:
- docs: bfloat16 [4096, 4, 896], P(('row', 'col')), may hold values from -6 to 6
- routes: int32 [4096, 1], P(('row', 'col')), may hold values from 0 to 31; in each aligned block of 128 rows (0 to 127, 128 to 255, ...) at most 8 rows name the same one
- level_one: float32 [4, 896, 896], P('row', 'col'), may hold values from -6 to 6
- level_two: float32 [8, 896, 896], P('col', 'row'), may hold values from -6 to 6
- moment_one: float32 [4, 896, 896], P('row', 'col'), may hold values from -18 to 18
- moment_two: float32 [8, 896, 896], P('col', 'row'), may hold values from -18 to 18
Outputs:
- new_one: float32 [4, 896, 896], P('row', 'col')
- new_two: float32 [8, 896, 896], P('col', 'row')
- next_moment_one: float32 [4, 896, 896], P('row', 'col')
- next_moment_two: float32 [8, 896, 896], P('col', 'row')
Inputs may be any that keep to these rules, and one draw needn't show every extreme that they name: `routes`: each block names one path; among the 128 blocks of one device no path is named more than 8 times, and every path is named by some block.
All inputs are finite; a program needn't handle non-finite values.
Results may differ from a plain program's by a relative error of at most 0.017.
Values may be sent and summed in bfloat16 or wider, within the bound.
A program may use at most 128 MiB of HBM per device.

v0:
```python
import functools

import jax
import jax.numpy as jnp
from jax import lax
from jax.experimental import pallas as pl
from jax.experimental.pallas import tpu as pltpu
from jax.sharding import PartitionSpec as P

STEPS = 3


inner_rate = 64.0
outer_rate = 0.7
momentum_decay = 0.9

MESH = pl.DeviceIdType.MESH


def normalize(values):
    return values * lax.rsqrt(jnp.mean(values * values, axis=-1, keepdims=True) + 1e-06)


def path_loss(weights, inputs, targets, total):
    first, second = weights
    factor = inputs.shape[-1] ** (-0.5)
    hidden_in = (
        jnp.dot(
            normalize(inputs).astype(jnp.bfloat16),
            first.astype(jnp.bfloat16),
            preferred_element_type=jnp.float32,
        )
        * factor
    )
    hidden = inputs + jax.nn.silu(hidden_in)
    output = (
        hidden
        + jnp.dot(
            normalize(hidden).astype(jnp.bfloat16),
            second.astype(jnp.bfloat16),
            preferred_element_type=jnp.float32,
        )
        * factor
    )
    error = output - targets
    return 0.5 * jnp.sum(error * error) / total


def train_path(first, second, inputs, targets, total):
    for turn in range(STEPS):
        grads = jax.grad(path_loss)((first, second), inputs, targets, total)
        first = first - inner_rate * grads[0]
        second = second - inner_rate * grads[1]
    return (first, second)


def exchange_kernel(
    n_row, n_col, line_ref, docs_ref, level_one_ref, level_two_ref,
    inputs, targets, total, whole_one, whole_two,
    arrived, counts, out_ref, cnt_ref, one_ref, two_ref,
    doc_send, doc_recv, cnt_send, cnt_recv, up_send, down_send, one_recv,
    pair_send, pair_recv, two_send, two_recv, local_sem,
):
    row, col = lax.axis_index("row"), lax.axis_index("col")
    n = n_row * n_col
    me = row * n_col + col
    chips = n_col // 2
    place, core = col // 2, col % 2
    lines, width = arrived.shape[1:]
    kept = inputs.shape[1]
    depth = docs_ref.shape[0]
    barrier = pltpu.get_barrier_semaphore()

    def greet(k, carry):
        to = (me + k) % n
        pl.semaphore_signal(
            barrier, inc=1, device_id={"row": to // n_col, "col": to % n_col}, device_id_type=MESH
        )
        return carry

    lax.fori_loop(1, n, greet, 0)
    one_ref[...] = level_one_ref[...].astype(jnp.bfloat16)
    two_ref[...] = level_two_ref[...].astype(jnp.bfloat16)
    pl.semaphore_wait(barrier, n - 1)

    def along(source, block, to, send):
        return pltpu.make_async_remote_copy(
            src_ref=source,
            dst_ref=whole_one.at[block],
            send_sem=send.at[block],
            recv_sem=one_recv.at[block],
            device_id={"row": row, "col": to},
            device_id_type=MESH,
        )

    def across(source, block):
        return pltpu.make_async_remote_copy(
            src_ref=source,
            dst_ref=whole_one.at[block],
            send_sem=pair_send.at[block],
            recv_sem=pair_recv.at[block],
            device_id={"row": row, "col": place * 2 + 1 - core},
            device_id_type=MESH,
        )

    @pl.when(place < chips - 1)
    def _():
        along(one_ref, col, col + 2, up_send).start()

    @pl.when(place > 0)
    def _():
        along(one_ref, col, col - 2, down_send).start()

    across(one_ref, col).start()

    def two_copy(k):
        to = (row + k) % n_row
        return pltpu.make_async_remote_copy(
            src_ref=two_ref,
            dst_ref=whole_two.at[row],
            send_sem=two_send.at[k],
            recv_sem=two_recv.at[k],
            device_id={"row": to, "col": col},
            device_id_type=MESH,
        )

    for k in range(1, n_row):
        two_copy(k).start()

    own = [
        pltpu.make_async_copy(one_ref, whole_one.at[col], local_sem.at[0]),
        pltpu.make_async_copy(two_ref, whole_two.at[row], local_sem.at[1]),
        pltpu.make_async_copy(out_ref.at[me], arrived.at[me], local_sem.at[2]),
        pltpu.make_async_copy(cnt_ref.at[me], counts.at[me], local_sem.at[3]),
    ]
    own[0].start()
    own[1].start()

    path = lax.broadcasted_iota(jnp.int32, (n, 1, depth), 0) * lines
    wide = jnp.broadcast_to(line_ref[...][None], (n, 1, depth))
    named = ((wide >= path) & (wide < path + lines)).astype(jnp.float32)
    cnt_ref[...] = jnp.broadcast_to(jnp.sum(named, axis=-1, keepdims=True), cnt_ref.shape)

    def pair_of(shift, turn):
        to_row, to_col = (row + shift) % n_row, (col + turn) % n_col
        to = to_row * n_col + to_col
        k = shift * n_col + turn
        peer = {"row": to_row, "col": to_col}
        return (
            pltpu.make_async_remote_copy(
                src_ref=out_ref.at[to],
                dst_ref=arrived.at[me],
                send_sem=doc_send.at[k],
                recv_sem=doc_recv.at[k],
                device_id=peer,
                device_id_type=MESH,
            ),
            pltpu.make_async_remote_copy(
                src_ref=cnt_ref.at[to],
                dst_ref=counts.at[me],
                send_sem=cnt_send.at[k],
                recv_sem=cnt_recv.at[k],
                device_id=peer,
                device_id_type=MESH,
            ),
        )

    def send_group(shift):
        to_row = (row + shift) % n_row
        base = to_row * n_col * lines
        index = lax.broadcasted_iota(jnp.int32, (n_col * lines, depth), 0) + base
        dispatch = (index == line_ref[...]).astype(jnp.float32).astype(jnp.bfloat16)
        rows = jnp.dot(dispatch, docs_ref[...], preferred_element_type=jnp.float32)
        out_ref[pl.ds(to_row * n_col, n_col)] = rows.reshape(n_col, lines, width).astype(
            jnp.bfloat16
        )

        def body(turn, carry):
            for copy in pair_of(shift, turn):
                copy.start()
            return carry

        lax.fori_loop(1 if shift == 0 else 0, n_col, body, 0)
        if shift == 0:
            own[2].start()
            own[3].start()

    for step in range(1, max(n_row, chips - 1) + 1):
        if step <= n_row:
            send_group(step % n_row)
        if step < chips:
            low, high = col - 2 * step, col + 2 * step

            @pl.when(place >= step)
            def _():
                along(one_ref, low, col, up_send).wait_recv()
                across(whole_one.at[low], low).start()

            @pl.when((place >= step) & (place < chips - 1))
            def _():
                along(whole_one.at[low], low, col + 2, up_send).start()

            @pl.when(place < chips - step)
            def _():
                along(one_ref, high, col, down_send).wait_recv()
                across(whole_one.at[high], high).start()

            @pl.when((place < chips - step) & (place > 0))
            def _():
                along(whole_one.at[high], high, col - 2, down_send).start()

    def unpack(source):
        rows = arrived[source].astype(jnp.float32)
        inputs[source] = rows[:kept]
        targets[source] = rows[lines - kept :]
        total[...] += counts[source]

    for copy in own:
        copy.wait()
    total[...] = jnp.zeros_like(total)
    unpack(me)

    for step in range(1, n_row + 1):
        shift = step % n_row

        def finish(turn, carry):
            for copy in pair_of(shift, turn):
                copy.wait()
            unpack((row - shift + n_row) % n_row * n_col + (col - turn + n_col) % n_col)
            return carry

        lax.fori_loop(1 if shift == 0 else 0, n_col, finish, 0)

    for q in range(chips):
        block = 2 * q + core
        across(one_ref, block).wait_send()
        across(one_ref, 2 * q + 1 - core).wait_recv()

        @pl.when((place >= q) & (place < chips - 1))
        def _():
            along(one_ref, block, col + 2, up_send).wait_send()

        @pl.when((place <= q) & (place > 0))
        def _():
            along(one_ref, block, col - 2, down_send).wait_send()

    for k in range(1, n_row):
        two_copy(k).wait()


def exchange(n_row, n_col, lines, kept, line, docs, level_one, level_two):
    n = n_row * n_col
    width = docs.shape[-1]
    vmem = pl.BlockSpec(memory_space=pltpu.VMEM)
    dma = pltpu.SemaphoreType.DMA
    return pl.pallas_call(
        functools.partial(exchange_kernel, n_row, n_col),
        out_shape=(
            jax.ShapeDtypeStruct((n, kept, width), jnp.float32),
            jax.ShapeDtypeStruct((n, kept, width), jnp.float32),
            jax.ShapeDtypeStruct((1, 128), jnp.float32),
            jax.ShapeDtypeStruct((n_col,) + level_one.shape, jnp.bfloat16),
            jax.ShapeDtypeStruct((n_row,) + level_two.shape, jnp.bfloat16),
        ),
        in_specs=[vmem] * 4,
        out_specs=(vmem,) * 5,
        scratch_shapes=[
            pltpu.VMEM((n, lines, width), jnp.bfloat16),
            pltpu.VMEM((n, 1, 128), jnp.float32),
            pltpu.VMEM((n, lines, width), jnp.bfloat16),
            pltpu.VMEM((n, 1, 128), jnp.float32),
            pltpu.VMEM(level_one.shape, jnp.bfloat16),
            pltpu.VMEM(level_two.shape, jnp.bfloat16),
            dma((n,)), dma((n,)), dma((n,)), dma((n,)),
            dma((n_col,)), dma((n_col,)), dma((n_col,)), dma((n_col,)), dma((n_col,)),
            dma((n_row,)), dma((n_row,)), dma((4,)),
        ],
        compiler_params=pltpu.CompilerParams(collective_id=0, has_side_effects=True),
    )(line, docs, level_one, level_two)


def scatter_kernel(
    n_row, n_col, one_ref, two_ref, share_one, share_two,
    pair_buf, part_buf, one_buf, two_buf,
    pair_send, pair_recv, one_send, one_recv, two_send, two_recv,
):
    row, col = lax.axis_index("row"), lax.axis_index("col")
    chips = n_col // 2
    place, core = col // 2, col % 2
    barrier = pltpu.get_barrier_semaphore()

    def greet(to_row, to_col):
        pl.semaphore_signal(
            barrier, inc=1, device_id={"row": to_row, "col": to_col}, device_id_type=MESH
        )

    partner = place * 2 + 1 - core
    greet(row, partner)
    for k in range(1, chips):
        greet(row, (col + 2 * k) % n_col)
    for k in range(1, n_row):
        greet((row + k) % n_row, col)
    pl.semaphore_wait(barrier, chips + n_row - 1)

    def pair_copy(q):
        return pltpu.make_async_remote_copy(
            src_ref=one_ref.at[2 * q + 1 - core],
            dst_ref=pair_buf.at[q],
            send_sem=pair_send.at[q],
            recv_sem=pair_recv.at[q],
            device_id={"row": row, "col": partner},
            device_id_type=MESH,
        )

    def two_copy(k):
        to = (row + k) % n_row
        return pltpu.make_async_remote_copy(
            src_ref=two_ref.at[to],
            dst_ref=two_buf.at[k],
            send_sem=two_send.at[k],
            recv_sem=two_recv.at[k],
            device_id={"row": to, "col": col},
            device_id_type=MESH,
        )

    def one_copy(k):
        return pltpu.make_async_remote_copy(
            src_ref=part_buf.at[k],
            dst_ref=one_buf.at[k],
            send_sem=one_send.at[k],
            recv_sem=one_recv.at[k],
            device_id={"row": row, "col": (col + 2 * k) % n_col},
            device_id_type=MESH,
        )

    for k in range(1, chips):
        pair_copy((place + k) % chips).start()
    pair_copy(place).start()
    for k in range(1, n_row):
        two_copy(k).start()
    for k in range(1, chips):
        q = (place + k) % chips
        pair_copy(q).wait_recv()
        part_buf[k] = (
            one_ref[2 * q + core].astype(jnp.float32) + pair_buf[q].astype(jnp.float32)
        ).astype(jnp.bfloat16)
        one_copy(k).start()
    pair_copy(place).wait_recv()
    share_one[...] = one_ref[col].astype(jnp.float32) + pair_buf[place].astype(jnp.float32)
    share_two[...] = two_ref[row].astype(jnp.float32)
    for k in range(1, chips):
        one_copy(k).wait_recv()
        share_one[...] += one_buf[k].astype(jnp.float32)
    for k in range(1, n_row):
        two_copy(k).wait_recv()
        share_two[...] += two_buf[k].astype(jnp.float32)
    for q in range(chips):
        pair_copy(q).wait_send()
    for k in range(1, chips):
        one_copy(k).wait_send()
    for k in range(1, n_row):
        two_copy(k).wait_send()


def scatter(n_row, n_col, change_one, change_two):
    width = change_one.shape[-1]
    chips = n_col // 2
    rows_one, rows_two = width // n_col, width // n_row
    vmem = pl.BlockSpec(memory_space=pltpu.VMEM)
    dma = pltpu.SemaphoreType.DMA
    return pl.pallas_call(
        functools.partial(scatter_kernel, n_row, n_col),
        out_shape=(
            jax.ShapeDtypeStruct((rows_one, width), jnp.float32),
            jax.ShapeDtypeStruct((rows_two, width), jnp.float32),
        ),
        in_specs=[vmem] * 2,
        out_specs=(vmem,) * 2,
        scratch_shapes=[
            pltpu.VMEM((chips, rows_one, width), jnp.bfloat16),
            pltpu.VMEM((chips, rows_one, width), jnp.bfloat16),
            pltpu.VMEM((chips, rows_one, width), jnp.bfloat16),
            pltpu.VMEM((n_row, rows_two, width), jnp.bfloat16),
            dma((chips,)), dma((chips,)), dma((chips,)), dma((chips,)),
            dma((n_row,)), dma((n_row,)),
        ],
        compiler_params=pltpu.CompilerParams(collective_id=1, has_side_effects=True),
    )(
        change_one.reshape(n_col, rows_one, width),
        change_two.reshape(n_row, rows_two, width),
    )


def shards(docs, routes, level_one, level_two, moment_one, moment_two):
    n_row = lax.axis_size("row")
    n_col = lax.axis_size("col")
    paths = n_row * n_col
    count = docs.shape[0]
    length = docs.shape[1]
    width = docs.shape[2]
    capacity = max(2, (2 * count + paths - 1) // paths)
    target = routes[:, 0]
    places = jnp.arange(count, dtype=jnp.int32)
    same = (target[:, None] == target[None, :]) & (places[None, :] < places[:, None])
    rank = jnp.sum(same.astype(jnp.int32), axis=1)
    steps = jnp.arange(length, dtype=jnp.int32)
    line = ((target * length * capacity + rank)[:, None] + steps[None, :] * capacity).reshape(-1)
    inputs, targets, filled, whole_one, whole_two = exchange(
        n_row,
        n_col,
        length * capacity,
        (length - 1) * capacity,
        line[None, :],
        docs.reshape(count * length, width),
        level_one[0],
        level_two[0],
    )
    total = filled[0, 0] * ((length - 1) / length)
    inputs = inputs.reshape(-1, width)
    targets = targets.reshape(-1, width)
    whole_one = whole_one.reshape(width, width).astype(jnp.float32)
    whole_two = whole_two.reshape(width, width).astype(jnp.float32)
    end_one, end_two = train_path(whole_one, whole_two, inputs, targets, total)
    share_one, share_two = scatter(
        n_row,
        n_col,
        (whole_one - end_one).astype(jnp.bfloat16),
        (whole_two - end_two).astype(jnp.bfloat16),
    )
    delta_one = (share_one / n_col)[None]
    delta_two = (share_two / n_row)[None]
    next_moment_one = momentum_decay * moment_one + delta_one
    next_moment_two = momentum_decay * moment_two + delta_two
    new_one = level_one - outer_rate * (delta_one + momentum_decay * next_moment_one)
    new_two = level_two - outer_rate * (delta_two + momentum_decay * next_moment_two)
    return (new_one, new_two, next_moment_one, next_moment_two)


def solution(mesh):
    placed = (
        P(("row", "col"), None, None),
        P(("row", "col"), None),
        P("row", "col", None),
        P("col", "row", None),
        P("row", "col", None),
        P("col", "row", None),
    )
    return jax.shard_map(
        shards,
        mesh=mesh,
        in_specs=placed,
        out_specs=(
            P("row", "col", None),
            P("col", "row", None),
            P("row", "col", None),
            P("col", "row", None),
        ),
        check_vma=False,
    )
```

profile of v0, /device:TPU:0, one launch (start us, length us, event | category | flops | bytes accessed | tf_op | source)
XLA Modules:
  0.0 139.7 jit_solution(11127128566230362309)
XLA Ops:
  0.6 0.9 convert_reduce_fusion
  1.5 0.7 fusion.123
  2.2 0.1 broadcast_add_fusion
  2.3 0.7 add.116.line_ref
  3.0 2.4 %reshape.135.docs_ref = bf16[512,896]{1,0:T(8,128)(2,1)} reshape(bf16[128,4,896]{2,1,0:T(4,128)(2,1)} %param.6) | data formatting | bytes 1835008 | tf_op jit(solution)/shard_map/reshape | solution.py:414
  5.4 61.9 %shard_map.93 = (f32[32,24,896]{2,1,0:T(8,128)}, f32[32,24,896]{2,1,0:T(8,128)}, f32[1,128]{1,0:T(1,128)}, bf16[8,112,896]{2,1,0:T(8,128)(2,1)}, bf16[4,224,896]{2,1,0:T(8,128)(2,1)}) custom-call(s32[1,512]{1,0:T(1,128)} %add.116.line_ref, bf16[512,896]{1,0:T(8,128)(2,1)} %reshape.135.docs_ref, f32[112,896]{1,0:T(8,128)} %bitcast.78, f32[224,896]{1,0:T(8,128)} %bitcast.75), custom_call_target="tpu_custom_call" | custom-call | tf_op jit(solution)/shard_map/pallas_call | solution.py:256
  67.3 0.0 copy-start.1
  68.2 2.0 %multiply_reduce_fusion.3 = f32[32,24]{1,0:T(8,128)S(1)} fusion(f32[32,24,896]{2,1,0:T(8,128)} %get-tuple-element.12), kind=kLoop, calls=%fused_computation.73 | loop fusion | flops 1375488 | bytes 2755584 | tf_op jit(solution)/shard_map/jvp()/reduce_sum | solution.py:21
  70.3 0.1 rsqrt.45
  70.3 0.0 copy-done.1
  70.4 0.0 copy-start.7
  70.4 0.2 multiply_convert_fusion.3
  70.6 1.2 copy-done.7
  71.8 0.0 copy-start
  71.8 0.0 copy-start.6
  71.8 2.4 %multiply_reduce_fusion.2 = (f32[768]{0:T(1024)S(1)}, f32[768,896]{1,0:T(8,128)S(1)}, bf16[768,896]{1,0:T(8,128)(2,1)S(1)}, f32[768,896]{1,0:T(8,128)S(1)}) fusion(f32[32,24,896]{2,1,0:T(8,128)S(1)} %copy-done.1, f32[768]{0:T(1024)S(1)} %rsqrt.45, bf16[768,896]{1,0:T(8,128)(2,1)S(1)} %bitcast.79, bf16[896,896]{1,0:T(8,128)(2,1)S(1)} %bitcast.80), kind=kOutput, calls=%fused_computation.70 | convolution fusion | flops 1240005888 | bytes 12621824 | tf_op jit(solution)/shard_map/jvp()/dot_general | solution.py:28
  74.2 0.0 copy-done
  74.2 0.0 copy-done.6
  74.3 1.8 %fusion.26 = f32[768,896]{1,0:T(8,128)S(1)} fusion(f32[32,24,896]{2,1,0:T(8,128)S(1)} %copy-done.6, f32[768,896]{1,0:T(8,128)S(1)} %get-tuple-element.27, bf16[896,896]{1,0:T(8,128)(2,1)S(1)} %bitcast.70, f32[]{:T(128)} %bitcast.10, f32[768]{0:T(1024)S(1)} %fusion.120), kind=kOutput, calls=%fused_computation.44 | convolution fusion | flops 1237942272 | bytes 9866244 | tf_op jit(solution)/shard_map/jvp()/dot_general | solution.py:38
  76.1 1.8 %fusion.5 = (f32[768]{0:T(1024)S(1)}, bf16[768,896]{1,0:T(8,128)(2,1)S(1)}) fusion(f32[768,896]{1,0:T(8,128)S(1)} %get-tuple-element.27, bf16[896,896]{1,0:T(8,128)(2,1)S(1)} %bitcast.71, f32[768,896]{1,0:T(8,128)S(1)} %fusion.26), kind=kOutput, calls=%fused_computation.23 | convolution fusion | flops 1236565248 | bytes 8489984 | tf_op jit(solution)/shard_map/transpose(jvp())/dot_general | solution.py:38
  78.0 2.8 %fusion.73 = bf16[896,896]{1,0:T(8,128)(2,1)S(1)} fusion(bf16[768,896]{1,0:T(8,128)(2,1)S(1)} %get-tuple-element.28, f32[768,896]{1,0:T(8,128)S(1)} %fusion.26, bf16[768,896]{1,0:T(8,128)(2,1)S(1)} %get-tuple-element.31, f32[768,896]{1,0:T(8,128)S(1)} %get-tuple-element.27, f32[768,896]{1,0:T(8,128)S(1)} %get-tuple-element.29, ...), kind=kOutput, calls=%fused_computation.96 | convolution fusion | flops 1245626368 | bytes 12621824 | tf_op jit(solution)/shard_map/transpose(jvp())/dot_general | solution.py:28
  80.7 1.7 %fusion.58 = bf16[896,896]{1,0:T(8,128)(2,1)S(1)} fusion(f32[768,896]{1,0:T(8,128)S(1)} %fusion.26, f32[768,896]{1,0:T(8,128)S(1)} %get-tuple-element.27, f32[768]{0:T(1024)S(1)} %fusion.120), kind=kOutput, calls=%fused_computation.91 | convolution fusion | flops 1235992576 | bytes 7113728 | tf_op jit(solution)/shard_map/transpose(jvp())/dot_general | solution.py:38
  82.5 2.5 %multiply_reduce_fusion.1 = (f32[768]{0:T(1024)S(1)}, f32[768,896]{1,0:T(8,128)S(1)}, f32[768,896]{1,0:T(8,128)S(1)}) fusion(f32[32,24,896]{2,1,0:T(8,128)S(1)} %copy-done.1, bf16[768,896]{1,0:T(8,128)(2,1)S(1)} %get-tuple-element.28, bf16[896,896]{1,0:T(8,128)(2,1)S(1)} %fusion.73, bf16[896,896]{1,0:T(8,128)(2,1)S(1)} %bitcast.81), kind=kOutput, calls=%fused_computation.64 | convolution fusion | flops 1242643712 | bytes 12848128 | tf_op jit(solution)/shard_map/jvp()/dot_general | solution.py:28
  85.0 1.9 %fusion.28 = f32[768,896]{1,0:T(8,128)S(1)} fusion(f32[32,24,896]{2,1,0:T(8,128)S(1)} %copy-done.6, f32[768,896]{1,0:T(8,128)S(1)} %get-tuple-element.25, f32[]{:T(128)} %bitcast.10, f32[768]{0:T(1024)S(1)} %fusion.121, bf16[896,896]{1,0:T(8,128)(2,1)S(1)} %fusion.58, bf16[896,896]{1,0:T(8,128)(2,1)S(1)} %bitcast.72), kind=kOutput, calls=%fused_computation.46 | convolution fusion | flops 1241956352 | bytes 11471876 | tf_op jit(solution)/shard_map/jvp()/dot_general | solution.py:38
  86.9 1.9 %fusion.7 = (f32[768]{0:T(1024)S(1)}, bf16[768,896]{1,0:T(8,128)(2,1)S(1)}) fusion(f32[768,896]{1,0:T(8,128)S(1)} %get-tuple-element.25, bf16[896,896]{1,0:T(8,128)(2,1)S(1)} %fusion.58, bf16[896,896]{1,0:T(8,128)(2,1)S(1)} %bitcast.73, f32[768,896]{1,0:T(8,128)S(1)} %fusion.28), kind=kOutput, calls=%fused_computation.25 | convolution fusion | flops 1240579328 | bytes 10095616 | tf_op jit(solution)/shard_map/transpose(jvp())/dot_general | solution.py:38
  88.8 2.8 %fusion.70 = bf16[896,896]{1,0:T(8,128)(2,1)S(1)} fusion(bf16[768,896]{1,0:T(8,128)(2,1)S(1)} %get-tuple-element.28, f32[768,896]{1,0:T(8,128)S(1)} %fusion.28, bf16[768,896]{1,0:T(8,128)(2,1)S(1)} %get-tuple-element.34, f32[768,896]{1,0:T(8,128)S(1)} %get-tuple-element.25, f32[768,896]{1,0:T(8,128)S(1)} %get-tuple-element.32, ...), kind=kOutput, calls=%fused_computation.95 | convolution fusion | flops 1245626368 | bytes 12621824 | tf_op jit(solution)/shard_map/transpose(jvp())/dot_general | solution.py:28
  91.6 2.1 %fusion.57 = (bf16[896,896]{1,0:T(8,128)(2,1)S(1)}, bf16[896,896]{1,0:T(8,128)(2,1)S(1)}) fusion(bf16[896,896]{1,0:T(8,128)(2,1)S(1)} %fusion.58, bf16[4,224,896]{2,1,0:T(8,128)(2,1)S(1)} %copy-done, f32[768,896]{1,0:T(8,128)S(1)} %fusion.28, f32[768,896]{1,0:T(8,128)S(1)} %get-tuple-element.25, f32[768]{0:T(1024)S(1)} %fusion.121), kind=kOutput, calls=%fused_computation.90 | convolution fusion | flops 1242415104 | bytes 11930624 | tf_op jit(solution)/shard_map/transpose(jvp())/dot_general | solution.py:38
  93.7 2.4 %multiply_reduce_fusion = (f32[768]{0:T(1024)S(1)}, f32[768,896]{1,0:T(8,128)S(1)}, f32[768,896]{1,0:T(8,128)S(1)}) fusion(f32[32,24,896]{2,1,0:T(8,128)S(1)} %copy-done.1, bf16[768,896]{1,0:T(8,128)(2,1)S(1)} %get-tuple-element.28, bf16[896,896]{1,0:T(8,128)(2,1)S(1)} %fusion.70, bf16[896,896]{1,0:T(8,128)(2,1)S(1)} %fusion.73, ...), kind=kOutput, calls=%fused_computation.58 | convolution fusion | flops 1245052160 | bytes 14453760 | tf_op jit(solution)/shard_map/jvp()/dot_general | solution.py:28
  96.1 1.8 %fusion.30 = f32[768,896]{1,0:T(8,128)S(1)} fusion(f32[32,24,896]{2,1,0:T(8,128)S(1)} %copy-done.6, f32[768,896]{1,0:T(8,128)S(1)} %get-tuple-element.23, bf16[896,896]{1,0:T(8,128)(2,1)S(1)} %get-tuple-element.36, f32[]{:T(128)} %bitcast.10, f32[768]{0:T(1024)S(1)} %fusion.122), kind=kOutput, calls=%fused_computation.48 | convolution fusion | flops 1237942272 | bytes 9866244 | tf_op jit(solution)/shard_map/jvp()/dot_general | solution.py:38
  97.9 3.9 %fusion.1 = bf16[896,896]{1,0:T(8,128)(2,1)} fusion(bf16[896,896]{1,0:T(8,128)(2,1)S(1)} %bitcast.74, bf16[896,896]{1,0:T(8,128)(2,1)S(1)} %get-tuple-element.37, bf16[896,896]{1,0:T(8,128)(2,1)S(1)} %fusion.58, f32[768,896]{1,0:T(8,128)S(1)} %fusion.30, f32[768,896]{1,0:T(8,128)S(1)} %get-tuple-element.23, f32[768]{0:T(1024)S(1)} %fusion.122), kind=kOutput, calls=%fused_computation.17 | convolution fusion | flops 1245626368 | bytes 11930624 | tf_op jit(solution)/shard_map/transpose(jvp())/dot_general | solution.py:38
  101.8 1.8 %fusion.9 = (f32[768]{0:T(1024)S(1)}, bf16[768,896]{1,0:T(8,128)(2,1)S(1)}) fusion(f32[768,896]{1,0:T(8,128)S(1)} %get-tuple-element.23, bf16[896,896]{1,0:T(8,128)(2,1)S(1)} %get-tuple-element.36, f32[768,896]{1,0:T(8,128)S(1)} %fusion.30), kind=kOutput, calls=%fused_computation.27 | convolution fusion | flops 1236565248 | bytes 8489984 | tf_op jit(solution)/shard_map/transpose(jvp())/dot_general | solution.py:38
  103.7 4.6 %fusion = bf16[896,896]{1,0:T(8,128)(2,1)} fusion(bf16[896,896]{1,0:T(8,128)(2,1)S(1)} %bitcast.83, bf16[896,896]{1,0:T(8,128)(2,1)S(1)} %fusion.70, bf16[896,896]{1,0:T(8,128)(2,1)S(1)} %fusion.73, bf16[768,896]{1,0:T(8,128)(2,1)S(1)} %get-tuple-element.28, f32[768,896]{1,0:T(8,128)S(1)} %fusion.30, bf16[768,896]{1,0:T(8,128)(2,1)S(1)} %get-tuple-element.39, ...), kind=kOutput, calls=%fused_computation.16 | convolution fusion | flops 1255260160 | bytes 17438720 | tf_op jit(solution)/shard_map/transpose(jvp())/dot_general | solution.py:28
  108.3 0.0 copy-start.3
  108.3 0.0 copy-start.5
  108.3 0.0 copy-start.2
  108.3 0.0 copy-start.4
  108.3 26.9 %shard_map.94 = (f32[112,896]{1,0:T(8,128)}, f32[224,896]{1,0:T(8,128)}) custom-call(bf16[8,112,896]{2,1,0:T(8,128)(2,1)} %bitcast.77, bf16[4,224,896]{2,1,0:T(8,128)(2,1)} %bitcast.76), custom_call_target="tpu_custom_call" | custom-call | tf_op jit(solution)/shard_map/pallas_call | solution.py:371
  135.2 0.0 copy-done.3
  135.2 0.0 copy-done.5
  135.2 2.0 %fusion.118 = (f32[1,112,896]{2,1,0:T(8,128)}, f32[1,112,896]{2,1,0:T(8,128)}) fusion(f32[1,112,896]{2,1,0:T(8,128)S(1)} %copy-done.3, f32[112,896]{1,0:T(8,128)} %get-tuple-element.16, f32[1,112,896]{2,1,0:T(8,128)S(1)} %copy-done.5), kind=kLoop, calls=%fused_computation.129 | loop fusion | flops 702464 | bytes 2007040 | tf_op jit(solution)/shard_map/sub | solution.py:434
  137.2 0.0 copy-done.2
  137.2 0.0 copy-done.4
  137.2 2.5 %fusion.114 = (f32[1,224,896]{2,1,0:T(8,128)}, f32[1,224,896]{2,1,0:T(8,128)}) fusion(f32[1,224,896]{2,1,0:T(8,128)S(1)} %copy-done.2, f32[224,896]{1,0:T(8,128)} %get-tuple-element.17, f32[1,224,896]{2,1,0:T(8,128)S(1)} %copy-done.4), kind=kLoop, calls=%fused_computation.125 | loop fusion | flops 1404928 | bytes 4014080 | tf_op jit(solution)/shard_map/sub | solution.py:435
  (8 shorter events, 0.1 us)
Async XLA Ops:
  67.3 3.0 %copy-start.1 = (f32[32,24,896]{2,1,0:T(8,128)S(1)}, f32[32,24,896]{2,1,0:T(8,128)}, u32[]{:S(2)}) copy-start(f32[32,24,896]{2,1,0:T(8,128)} %get-tuple-element.12) | copy-start | bytes 8257540
  70.4 1.4 %copy-start.7 = (bf16[8,112,896]{2,1,0:T(8,128)(2,1)S(1)}, bf16[8,112,896]{2,1,0:T(8,128)(2,1)}, u32[]{:S(2)}) copy-start(bf16[8,112,896]{2,1,0:T(8,128)(2,1)} %get-tuple-element.11) | copy-start | bytes 4816900
  71.8 2.5 %copy-start = (bf16[4,224,896]{2,1,0:T(8,128)(2,1)S(1)}, bf16[4,224,896]{2,1,0:T(8,128)(2,1)}, u32[]{:S(2)}) copy-start(bf16[4,224,896]{2,1,0:T(8,128)(2,1)} %get-tuple-element.13) | copy-start | bytes 4816900
  71.8 2.5 %copy-start.6 = (f32[32,24,896]{2,1,0:T(8,128)S(1)}, f32[32,24,896]{2,1,0:T(8,128)}, u32[]{:S(2)}) copy-start(f32[32,24,896]{2,1,0:T(8,128)} %get-tuple-element.14) | copy-start | bytes 8257540
  108.3 26.9 %copy-start.3 = (f32[1,112,896]{2,1,0:T(8,128)S(1)}, f32[1,112,896]{2,1,0:T(8,128)}, u32[]{:S(2)}) copy-start(f32[1,112,896]{2,1,0:T(8,128)} %param.8) | copy-start | bytes 1204228
  108.3 27.0 %copy-start.5 = (f32[1,112,896]{2,1,0:T(8,128)S(1)}, f32[1,112,896]{2,1,0:T(8,128)}, u32[]{:S(2)}) copy-start(f32[1,112,896]{2,1,0:T(8,128)} %param.10) | copy-start | bytes 1204228
  108.3 29.0 %copy-start.2 = (f32[1,224,896]{2,1,0:T(8,128)S(1)}, f32[1,224,896]{2,1,0:T(8,128)}, u32[]{:S(2)}) copy-start(f32[1,224,896]{2,1,0:T(8,128)} %param.9) | copy-start | bytes 2408452
  108.3 29.0 %copy-start.4 = (f32[1,224,896]{2,1,0:T(8,128)S(1)}, f32[1,224,896]{2,1,0:T(8,128)}, u32[]{:S(2)}) copy-start(f32[1,224,896]{2,1,0:T(8,128)} %param.11) | copy-start | bytes 2408452
where the time goes:
time: 140 us
  Pallas kernels  88.9 us (64%)
  matrix products  36.3 us (26%)
  other arithmetic  8.46 us (6%)
  local copies, waits for them, and re-layouts  4.39 us (3%)
  between operations  1.7 us (1%)
    pallas_call x1, Pallas kernels, exchange(): pl.pallas_call(functools.partial(exchange_kernel, n_row, n_col), out_shap...  61.9 us
    pallas_call x1, Pallas kernels, scatter(): pl.pallas_call(functools.partial(scatter_kernel, n_row, n_col), out_shape...  26.9 us
    dot_general x9, matrix products, path_loss(): jnp.dot(normalize(hidden).astype(jnp.bfloat16), second.astype(jnp.bfloat1...  18.8 us
    dot_general x6, matrix products, path_loss(): jnp.dot(normalize(inputs).astype(jnp.bfloat16), first.astype(jnp.bfloat16...  17.5 us

commit v1 on v0

v1 whole, which is shorter than its diff:
```python
import functools

import jax
import jax.numpy as jnp
from jax import lax
from jax.experimental import pallas as pl
from jax.experimental.pallas import tpu as pltpu
from jax.sharding import PartitionSpec as P

STEPS = 3
BLOCK_COLS = 256
EARLY = 4

inner_rate = 64.0
outer_rate = 0.7
momentum_decay = 0.9

MESH = pl.DeviceIdType.MESH
f32 = jnp.float32
bf16 = jnp.bfloat16


def product(a, b, i, j):
    return lax.dot_general(a, b, (((i,), (j,)), ((), ())), preferred_element_type=f32)


def column_blocks(width):
    return [(at, min(BLOCK_COLS, width - at)) for at in range(0, width, BLOCK_COLS)]


def fold(values):
    return sum(values[:, at : at + 128] for at in range(0, values.shape[1], 128))


def spread(values, width):
    return jnp.concatenate([values] * (width // 128), axis=1) if width > 128 else values


def round_kernel(
    n_row, n_col, cap, kept,
    route_ref, docs_hbm, one_hbm, two_hbm,
    share_one, share_two,
    docs_v, one_v, two_v, out_ref, cnt_ref, arrived, counts, whole_one, whole_two,
    z, h, g, e, ds, t, xb, hb, eb, db, gram, w2, dw, rx, rr, mm,
    one_out, two_out, pair_buf, part_buf, one_buf, two_buf,
    load_sem, doc_send, doc_recv, cnt_send, cnt_recv,
    up_send, down_send, one_recv, pair_send, pair_recv, two_send, two_recv,
    spair_send, spair_recv, sone_send, sone_recv, stwo_send, stwo_recv,
):
    row, col = lax.axis_index("row"), lax.axis_index("col")
    n = n_row * n_col
    me = row * n_col + col
    chips = n_col // 2
    place, core = col // 2, col % 2
    partner = place * 2 + 1 - core
    lines, width = arrived.shape[1:]
    rows = z.shape[0]
    per = rows // n
    group = 2 * n_row
    chunk = group * per
    half = rows // 2
    count = docs_v.shape[0]
    length = docs_v.shape[1]
    scale = width ** (-0.5)
    blocks = column_blocks(width)
    barrier = pltpu.get_barrier_semaphore()

    loads = [
        pltpu.make_async_copy(one_hbm, one_v, load_sem.at[0]),
        pltpu.make_async_copy(two_hbm, two_v, load_sem.at[1]),
        pltpu.make_async_copy(docs_hbm, docs_v, load_sem.at[2]),
    ]
    for copy in loads:
        copy.start()

    def greet(k, carry):
        to = (me + k) % n
        pl.semaphore_signal(
            barrier, inc=1, device_id={"row": to // n_col, "col": to % n_col}, device_id_type=MESH
        )
        return carry

    lax.fori_loop(1, n, greet, 0)
    loads[0].wait()
    whole_one[col] = one_v[...].astype(bf16)
    loads[1].wait()
    whole_two[row] = two_v[...].astype(bf16)

    target = route_ref[...]
    named = jnp.broadcast_to(target.astype(f32), (count, count))
    earlier = lax.broadcasted_iota(jnp.int32, (count, count), 0) < lax.broadcasted_iota(
        jnp.int32, (count, count), 1
    )
    rank = jnp.sum(jnp.where((named.T == named) & earlier, 1.0, 0.0), axis=0, keepdims=True)
    slot = target * cap + rank.astype(jnp.int32)
    slots = lax.broadcasted_iota(jnp.int32, (n * cap, count), 0)
    dispatch = jnp.where(slots == slot, 1.0, 0.0).astype(bf16)
    path = lax.broadcasted_iota(jnp.int32, (n, 1, count), 0)
    mine = jnp.where(jnp.broadcast_to(target[None], (n, 1, count)) == path, 1.0, 0.0)
    cnt_ref[...] = jnp.broadcast_to(jnp.sum(mine, axis=-1, keepdims=True), cnt_ref.shape)

    pl.semaphore_wait(barrier, n - 1)

    def along(block, to, send):
        return pltpu.make_async_remote_copy(
            src_ref=whole_one.at[block],
            dst_ref=whole_one.at[block],
            send_sem=send.at[block],
            recv_sem=one_recv.at[block],
            device_id={"row": row, "col": to},
            device_id_type=MESH,
        )

    def across(block):
        return pltpu.make_async_remote_copy(
            src_ref=whole_one.at[block],
            dst_ref=whole_one.at[block],
            send_sem=pair_send.at[block],
            recv_sem=pair_recv.at[block],
            device_id={"row": row, "col": partner},
            device_id_type=MESH,
        )

    def two_copy(k):
        return pltpu.make_async_remote_copy(
            src_ref=whole_two.at[row],
            dst_ref=whole_two.at[row],
            send_sem=two_send.at[k],
            recv_sem=two_recv.at[k],
            device_id={"row": (row + k) % n_row, "col": col},
            device_id_type=MESH,
        )

    def two_wait(k):
        from_row = (row - k + n_row) % n_row
        return pltpu.make_async_remote_copy(
            src_ref=whole_two.at[row],
            dst_ref=whole_two.at[from_row],
            send_sem=two_send.at[k],
            recv_sem=two_recv.at[k],
            device_id={"row": (row + k) % n_row, "col": col},
            device_id_type=MESH,
        )

    @pl.when(place < chips - 1)
    def _():
        along(col, col + 2, up_send).start()

    @pl.when(place > 0)
    def _():
        along(col, col - 2, down_send).start()

    across(col).start()
    for k in range(1, n_row):
        two_copy(k).start()

    loads[2].wait()
    docs = jnp.swapaxes(docs_v[...], 0, 1)
    for step in range(length):
        sent = jnp.dot(dispatch, docs[step], preferred_element_type=f32)
        out_ref[:, step * cap : (step + 1) * cap, :] = sent.reshape(n, cap, width).astype(bf16)

    def pair_of(u):
        to_row = (row + u % n_row) % n_row
        apart = u // group * 2 % chips + u // group // (chips // 2)
        to_col = (place + apart) % chips * 2 + (core + u // n_row) % 2
        to = to_row * n_col + to_col
        peer = {"row": to_row, "col": to_col}
        return (
            pltpu.make_async_remote_copy(
                src_ref=out_ref.at[to],
                dst_ref=arrived.at[u],
                send_sem=doc_send.at[u],
                recv_sem=doc_recv.at[u],
                device_id=peer,
                device_id_type=MESH,
            ),
            pltpu.make_async_remote_copy(
                src_ref=cnt_ref.at[to],
                dst_ref=counts.at[u],
                send_sem=cnt_send.at[u],
                recv_sem=cnt_recv.at[u],
                device_id=peer,
                device_id_type=MESH,
            ),
        )

    def send_docs(first, last):
        def body(u, carry):
            for copy in pair_of(u):
                copy.start()
            return carry

        lax.fori_loop(first, last, body, 0)

    arrived[0] = out_ref[me]
    counts[0] = cnt_ref[me]
    send_docs(1, group)
    pieces = [(at, min(at + EARLY, n)) for at in range(group, n, EARLY)]

    for step in range(1, chips):
        if pieces:
            send_docs(*pieces.pop(0))
        low, high = col - 2 * step, col + 2 * step

        @pl.when(place >= step)
        def _():
            along(low, col, up_send).wait_recv()
            across(low).start()

        @pl.when((place >= step) & (place < chips - 1))
        def _():
            along(low, col + 2, up_send).start()

        @pl.when(place < chips - step)
        def _():
            along(high, col, down_send).wait_recv()
            across(high).start()

        @pl.when((place < chips - step) & (place > 0))
        def _():
            along(high, col - 2, down_send).start()

    if pieces:
        send_docs(pieces[0][0], n)

    for q in range(chips):
        across(2 * q + 1 - core).wait_recv()
    for k in range(1, n_row):
        two_wait(k).wait_recv()

    def arrive(first, last):
        def body(u, carry):
            for copy in pair_of(u):
                copy.wait_recv()
            return carry

        lax.fori_loop(first, last, body, 0)

    def unpack(k, at):
        block = arrived[pl.ds(k * group, group)].astype(f32)
        if per == kept:
            first, last = block[:, :kept], block[:, lines - kept :]
        else:
            live = lax.broadcasted_iota(jnp.int32, block.shape, 1) < kept
            first = jnp.where(live, block, 0.0)[:, :per]
            last = jnp.where(live, pltpu.roll(block, kept, 1), 0.0)[:, :per]
        first = first.reshape(chunk, width)
        xb[at, :] = first.astype(bf16)
        t[at, :] = last.reshape(chunk, width).astype(bf16)
        size = jnp.sum(fold(first * first), axis=-1, keepdims=True) * (1.0 / width)
        rx[at, :] = jnp.broadcast_to(lax.rsqrt(size + 1e-06), (chunk, 128))

    def hidden(at, start):
        size = jnp.zeros((at.size, 128), f32)
        for n0, nn in blocks:
            cols = pl.ds(n0, nn)
            zz = start(cols, nn)
            z[at, cols] = zz
            gate = 1.0 / (1.0 + jnp.exp(-zz))
            act = zz * gate
            hh = xb[at, cols].astype(f32) + act
            h[at, cols] = hh
            hb[at, cols] = hh.astype(bf16)
            g[at, cols] = gate + act * (1.0 - gate)
            size = size + fold(hh * hh)
        size = jnp.sum(size, axis=-1, keepdims=True) * (1.0 / width)
        rr[at, :] = jnp.broadcast_to(lax.rsqrt(size + 1e-06), (at.size, 128))

    def errors(at, weights):
        r = rr[at, :]
        both = jnp.zeros((at.size, 128), f32)
        for n0, nn in blocks:
            cols = pl.ds(n0, nn)
            pp = product(hb[at, :], weights(cols), 1, 0)
            rw = spread(r, nn)
            ee = h[at, cols] + scale * rw * pp - t[at, cols].astype(f32)
            er = ee * rw
            e[at, cols] = ee
            eb[at, cols] = er.astype(bf16)
            both = both + fold(er * pp)
        both = jnp.sum(both, axis=-1, keepdims=True) * (1.0 / width)
        mm[at, :] = jnp.broadcast_to(both, (at.size, 128)) * r * r

    def slopes(at, weights, turn):
        m, rw = mm[at, :], rx[at, :]
        for n0, nn in blocks:
            cols = pl.ds(n0, nn)
            qq = product(eb[at, :], weights(cols), 1, 1)
            dd = (e[at, cols] + scale * (qq - h[at, cols] * spread(m, nn))) * g[at, cols]
            dd = dd * spread(rw, nn)
            if turn is None:
                ds[at, cols] = dd
                db[at, cols] = dd.astype(bf16)
            else:
                total = ds[at, cols] + dd
                ds[at, cols] = total
                db[at, cols] = jnp.where(turn == STEPS - 1, total, dd).astype(bf16)


    def two_cols(cols):
        return whole_two[:, :, cols].reshape(width, cols.size)

    def two_rows(cols):
        return whole_two[...].reshape(width, width)[cols.start : cols.start + cols.size]

    arrive(1, group)
    low, high = pl.ds(0, half), pl.ds(half, half)

    def first_turn(k, carry):
        at = pl.ds(pl.multiple_of(k * chunk, chunk), chunk)
        unpack(k, at)

        def start(cols, nn):
            zz = product(xb[at, :], whole_one[:, :, cols].reshape(width, nn), 1, 0)
            return scale * spread(rx[at, :], nn) * zz

        hidden(at, start)
        errors(at, two_cols)
        slopes(at, two_rows, None)

        @pl.when(k == chips // 2 - 1)
        def _():
            gram[low, low] = product(xb[low, :], xb[low, :], 1, 1).astype(bf16)
            for n0, nn in blocks:
                cols = pl.ds(n0, nn)
                dw[:, cols] = product(hb[low, :], eb[low, cols], 0, 0)

        @pl.when(k < chips - 1)
        def _():
            arrive((k + 1) * group, (k + 2) * group)

        return carry

    lax.fori_loop(0, chips, first_turn, 0)
    gram[high, :] = product(xb[high, :], xb[...], 1, 1).astype(bf16)
    gram[low, high] = product(xb[low, :], xb[high, :], 1, 1).astype(bf16)

    filled = jnp.sum(counts[...].reshape(n, 128), axis=0, keepdims=True)[:, :1]
    rate = inner_rate * scale / (filled * (length - 1))

    for n0, nn in blocks:
        cols = pl.ds(n0, nn)
        change = dw[:, cols] + product(hb[high, :], eb[high, cols], 0, 0)
        dw[:, cols] = change
        w2[1, :, cols] = (two_cols(cols).astype(f32) - rate * change).astype(bf16)

    everything = pl.ds(0, rows)

    def stwo_copy(k):
        to = (row + k) % n_row
        return pltpu.make_async_remote_copy(
            src_ref=two_out.at[to],
            dst_ref=two_buf.at[k],
            send_sem=stwo_send.at[k],
            recv_sem=stwo_recv.at[k],
            device_id={"row": to, "col": col},
            device_id_type=MESH,
        )

    def later_turn(turn, carry):
        now, later = turn % 2, (turn + 1) % 2

        def start(cols, nn):
            step = product(gram[...], db[:, cols], 1, 0)
            return z[:, cols] - (rate * scale) * spread(rx[...], nn) * step

        hidden(everything, start)
        errors(everything, lambda cols: w2[now, :, cols])
        for n0, nn in blocks:
            cols = pl.ds(n0, nn)
            change = dw[:, cols] + product(hb[...], eb[:, cols], 0, 0)
            dw[:, cols] = change
            change = rate * change
            w2[later, :, cols] = (two_cols(cols).astype(f32) - change).astype(bf16)
            two_out[:, :, cols] = change.astype(bf16).reshape(n_row, width // n_row, nn)

        @pl.when(turn == STEPS - 1)
        def _():
            for k in range(1, n_row):
                stwo_copy(k).start()

        slopes(everything, lambda cols: w2[now, cols, :], turn)
        return carry

    lax.fori_loop(1, STEPS, later_turn, 0)

    for n0, nn in blocks:
        cols = pl.ds(n0, nn)
        change = rate * product(xb[...], db[:, cols], 0, 0)
        one_out[:, :, cols] = change.astype(bf16).reshape(n_col, width // n_col, nn)

    def spair_copy(q):
        return pltpu.make_async_remote_copy(
            src_ref=one_out.at[2 * q + 1 - core],
            dst_ref=pair_buf.at[q],
            send_sem=spair_send.at[q],
            recv_sem=spair_recv.at[q],
            device_id={"row": row, "col": partner},
            device_id_type=MESH,
        )

    def sone_copy(k):
        return pltpu.make_async_remote_copy(
            src_ref=part_buf.at[k],
            dst_ref=one_buf.at[k],
            send_sem=sone_send.at[k],
            recv_sem=sone_recv.at[k],
            device_id={"row": row, "col": (col + 2 * k) % n_col},
            device_id_type=MESH,
        )

    for k in range(1, chips):
        spair_copy((place + k) % chips).start()
    spair_copy(place).start()
    for k in range(1, chips):
        q = (place + k) % chips
        spair_copy(q).wait_recv()
        part_buf[k] = (one_out[2 * q + core].astype(f32) + pair_buf[q].astype(f32)).astype(bf16)
        sone_copy(k).start()
    spair_copy(place).wait_recv()
    share_one[...] = one_out[col].astype(f32) + pair_buf[place].astype(f32)
    share_two[...] = two_out[row].astype(f32)
    for k in range(1, n_row):
        stwo_copy(k).wait_recv()
        share_two[...] += two_buf[k].astype(f32)
    for k in range(1, chips):
        sone_copy(k).wait_recv()
        share_one[...] += one_buf[k].astype(f32)

    def sent(u, carry):
        for copy in pair_of(u):
            copy.wait_send()
        return carry

    lax.fori_loop(1, n, sent, 0)
    for q in range(chips):
        block = 2 * q + core
        across(block).wait_send()

        @pl.when((place >= q) & (place < chips - 1))
        def _():
            along(block, col + 2, up_send).wait_send()

        @pl.when((place <= q) & (place > 0))
        def _():
            along(block, col - 2, down_send).wait_send()

        spair_copy(q).wait_send()
    for k in range(1, n_row):
        two_copy(k).wait_send()
        stwo_copy(k).wait_send()
    for k in range(1, chips):
        sone_copy(k).wait_send()


def shards(docs, routes, level_one, level_two, moment_one, moment_two):
    n_row = lax.axis_size("row")
    n_col = lax.axis_size("col")
    paths = n_row * n_col
    count, length, width = docs.shape
    cap = max(2, (2 * count + paths - 1) // paths)
    lines = length * cap
    kept = (length - 1) * cap
    per = (kept + 7) // 8 * 8
    rows = paths * per
    chips = n_col // 2
    one_rows, two_rows = width // n_col, width // n_row
    vmem = pl.BlockSpec(memory_space=pltpu.VMEM)
    hbm = pl.BlockSpec(memory_space=pl.ANY)
    dma = pltpu.SemaphoreType.DMA
    full = pltpu.VMEM((rows, width), f32)
    thin = pltpu.VMEM((rows, width), bf16)
    side = pltpu.VMEM((rows, 128), f32)
    share_one, share_two = pl.pallas_call(
        functools.partial(round_kernel, n_row, n_col, cap, kept),
        out_shape=(
            jax.ShapeDtypeStruct((one_rows, width), f32),
            jax.ShapeDtypeStruct((two_rows, width), f32),
        ),
        in_specs=[vmem, hbm, hbm, hbm],
        out_specs=(vmem,) * 2,
        scratch_shapes=[
            pltpu.VMEM((count, length, width), bf16),
            pltpu.VMEM((one_rows, width), f32),
            pltpu.VMEM((two_rows, width), f32),
            pltpu.VMEM((paths, lines, width), bf16),
            pltpu.VMEM((paths, 1, 128), f32),
            pltpu.VMEM((paths, lines, width), bf16),
            pltpu.VMEM((paths, 1, 128), f32),
            pltpu.VMEM((n_col, one_rows, width), bf16),
            pltpu.VMEM((n_row, two_rows, width), bf16),
            full, full, full, full, full, thin, thin, thin, thin, thin,
            pltpu.VMEM((rows, rows), bf16),
            pltpu.VMEM((2, width, width), bf16),
            pltpu.VMEM((width, width), f32),
            side, side, side,
            pltpu.VMEM((n_col, one_rows, width), bf16),
            pltpu.VMEM((n_row, two_rows, width), bf16),
            pltpu.VMEM((chips, one_rows, width), bf16),
            pltpu.VMEM((chips, one_rows, width), bf16),
            pltpu.VMEM((chips, one_rows, width), bf16),
            pltpu.VMEM((n_row, two_rows, width), bf16),
            dma((3,)), dma((paths,)), dma((paths,)), dma((paths,)), dma((paths,)),
            dma((n_col,)), dma((n_col,)), dma((n_col,)), dma((n_col,)), dma((n_col,)),
            dma((n_row,)), dma((n_row,)),
            dma((chips,)), dma((chips,)), dma((chips,)), dma((chips,)),
            dma((n_row,)), dma((n_row,)),
        ],
        compiler_params=pltpu.CompilerParams(
            collective_id=0, has_side_effects=True, vmem_limit_bytes=67043328
        ),
    )(routes.reshape(1, count), docs, level_one[0], level_two[0])
    delta_one = (share_one / n_col)[None]
    delta_two = (share_two / n_row)[None]
    next_moment_one = momentum_decay * moment_one + delta_one
    next_moment_two = momentum_decay * moment_two + delta_two
    new_one = level_one - outer_rate * (delta_one + momentum_decay * next_moment_one)
    new_two = level_two - outer_rate * (delta_two + momentum_decay * next_moment_two)
    return (new_one, new_two, next_moment_one, next_moment_two)


def solution(mesh):
    placed = (
        P(("row", "col"), None, None),
        P(("row", "col"), None),
        P("row", "col", None),
        P("col", "row", None),
        P("row", "col", None),
        P("col", "row", None),
    )
    return jax.shard_map(
        shards,
        mesh=mesh,
        in_specs=placed,
        out_specs=(
            P("row", "col", None),
            P("col", "row", None),
            P("row", "col", None),
            P("col", "row", None),
        ),
        check_vma=False,
    )
```

time: 140 us -> 112 us (0.80)
  the two profiles are of different devices: /device:TPU:0 before, /device:TPU:16 now
where the time goes in v1:
time: 112 us
  Pallas kernels  107 us (96%)
  other arithmetic  4.06 us (4%)
    pallas_call x1, Pallas kernels, shards(): pl.pallas_call(functools.partial(round_kernel, n_row, n_col, cap, kept),...  107 us
    sub x1, other arithmetic, shards(): level_two - outer_rate * (delta_two + momentum_decay * next_moment_two)  3.07 us

profile of v1, /device:TPU:16, one launch (start us, length us, event | category | flops | bytes accessed | tf_op | source)
XLA Modules:
  0.0 111.6 jit_solution(14321522503883418554)
XLA Ops:
  0.6 106.8 %shard_map.93 = (f32[112,896]{1,0:T(8,128)}, f32[224,896]{1,0:T(8,128)}) custom-call(s32[1,128]{1,0:T(1,128)} %bitcast.21, bf16[128,4,896]{2,1,0:T(4,128)(2,1)} %docs_hbm.1, f32[112,896]{1,0:T(8,128)} %bitcast.20, f32[224,896]{1,0:T(8,128)} %bitcast.19), custom_call_target="tpu_custom_call" | custom-call | tf_op jit(solution)/shard_map/pallas_call | solution.py:475
  107.5 0.0 copy-start
  107.5 0.0 copy-start.1
  107.5 0.0 copy-start.2
  107.5 3.1 %fusion.1 = (f32[1,224,896]{2,1,0:T(8,128)}, f32[1,224,896]{2,1,0:T(8,128)}) fusion(f32[1,224,896]{2,1,0:T(8,128)} %param.9, f32[224,896]{1,0:T(8,128)} %get-tuple-element.7, f32[1,224,896]{2,1,0:T(8,128)} %param.11), kind=kLoop, calls=%fused_computation.3 | loop fusion | flops 1404928 | bytes 4014080 | tf_op jit(solution)/shard_map/sub | solution.py:519
  110.6 0.0 copy-done
  110.6 0.0 copy-done.1
  110.6 0.0 copy-done.2
  110.6 1.0 fusion.3
Async XLA Ops:
  107.5 3.1 %copy-start = (f32[1,112,896]{2,1,0:T(8,128)S(1)}, f32[1,112,896]{2,1,0:T(8,128)}, u32[]{:S(2)}) copy-start(f32[1,112,896]{2,1,0:T(8,128)} %param.8) | copy-start | bytes 1204228
  107.5 3.1 %copy-start.1 = (f32[1,112,896]{2,1,0:T(8,128)S(1)}, f32[1,112,896]{2,1,0:T(8,128)}, u32[]{:S(2)}) copy-start(f32[1,112,896]{2,1,0:T(8,128)} %param.10) | copy-start | bytes 1204228
  107.5 3.1 %copy-start.2 = (f32[112,896]{1,0:T(8,128)S(1)}, f32[112,896]{1,0:T(8,128)}, u32[]{:S(2)}) copy-start(f32[112,896]{1,0:T(8,128)} %get-tuple-element.6) | copy-start | bytes 1204228

commit v2 on v1

--- a/solution.py
+++ b/solution.py
@@ -9,7 +9,6 @@
 
 STEPS = 3
 BLOCK_COLS = 256
-EARLY = 4
 
 inner_rate = 64.0
 outer_rate = 0.7
@@ -38,13 +37,13 @@
 
 def round_kernel(
     n_row, n_col, cap, kept,
-    route_ref, docs_hbm, one_hbm, two_hbm,
-    share_one, share_two,
-    docs_v, one_v, two_v, out_ref, cnt_ref, arrived, counts, whole_one, whole_two,
-    z, h, g, e, ds, t, xb, hb, eb, db, gram, w2, dw, rx, rr, mm,
-    one_out, two_out, pair_buf, part_buf, one_buf, two_buf,
+    route_ref, docs_hbm, one_hbm, two_hbm, moment_one_hbm, moment_two_hbm,
+    new_one, new_two, next_one, next_two,
+    docs_v, one_v, two_v, moment_one, moment_two, out_ref, cnt_ref, arrived, counts, whole_one, whole_two,
+    z, h, g, e, ds, t, xb, hb, eb, db, gram, w2, dw, rx, rr,
+    one_out, two_out, pair_buf, one_buf, two_buf,
     load_sem, doc_send, doc_recv, cnt_send, cnt_recv,
-    up_send, down_send, one_recv, pair_send, pair_recv, two_send, two_recv,
+    own_send, relay_send, one_recv, pair_send, pair_recv, two_send, two_recv,
     spair_send, spair_recv, sone_send, sone_recv, stwo_send, stwo_recv,
 ):
     row, col = lax.axis_index("row"), lax.axis_index("col")
@@ -53,6 +52,11 @@
     chips = n_col // 2
     place, core = col // 2, col % 2
     partner = place * 2 + 1 - core
+    side = chips // 2
+    upper = place // side
+    base = upper * side
+    entry = side - 1 + upper
+    other_entry = side - upper
     lines, width = arrived.shape[1:]
     rows = z.shape[0]
     per = rows // n
@@ -69,6 +73,8 @@
         pltpu.make_async_copy(one_hbm, one_v, load_sem.at[0]),
         pltpu.make_async_copy(two_hbm, two_v, load_sem.at[1]),
         pltpu.make_async_copy(docs_hbm, docs_v, load_sem.at[2]),
+        pltpu.make_async_copy(moment_one_hbm, moment_one, load_sem.at[3]),
+        pltpu.make_async_copy(moment_two_hbm, moment_two, load_sem.at[4]),
     ]
     for copy in loads:
         copy.start()
@@ -101,15 +107,32 @@
 
     pl.semaphore_wait(barrier, n - 1)
 
-    def along(block, to, send):
+    def own_copy(to):
+        return pltpu.make_async_remote_copy(
+            src_ref=whole_one.at[col],
+            dst_ref=whole_one.at[col],
+            send_sem=own_send.at[to],
+            recv_sem=one_recv.at[col],
+            device_id={"row": row, "col": 2 * to + core},
+            device_id_type=MESH,
+        )
+
+    def relay(source, to):
+        block = 2 * source + core
         return pltpu.make_async_remote_copy(
             src_ref=whole_one.at[block],
             dst_ref=whole_one.at[block],
-            send_sem=send.at[block],
+            send_sem=relay_send.at[source, to],
             recv_sem=one_recv.at[block],
-            device_id={"row": row, "col": to},
-            device_id_type=MESH,
-        )
+            device_id={"row": row, "col": 2 * to + core},
+            device_id_type=MESH,
+        )
+
+    def sibling(j):
+        return base + (place - base + j) % side
+
+    def beyond(i):
+        return (1 - upper) * (side + i) + upper * (side - 1 - i)
 
     def across(block):
         return pltpu.make_async_remote_copy(
@@ -142,14 +165,9 @@
             device_id_type=MESH,
         )
 
-    @pl.when(place < chips - 1)
-    def _():
-        along(col, col + 2, up_send).start()
-
-    @pl.when(place > 0)
-    def _():
-        along(col, col - 2, down_send).start()
-
+    own_copy(other_entry).start()
+    for j in range(1, side):
+        own_copy(sibling(j)).start()
     across(col).start()
     for k in range(1, n_row):
         two_copy(k).start()
@@ -162,8 +180,7 @@
 
     def pair_of(u):
         to_row = (row + u % n_row) % n_row
-        apart = u // group * 2 % chips + u // group // (chips // 2)
-        to_col = (place + apart) % chips * 2 + (core + u // n_row) % 2
+        to_col = (place + u // group) % chips * 2 + (core + u // n_row) % 2
         to = to_row * n_col + to_col
         peer = {"row": to_row, "col": to_col}
         return (
@@ -185,6 +202,10 @@
             ),
         )
 
+    def apart(k, flip):
+        near = k * 2 % chips + k // (chips // 2)
+        return (near + flip * (chips - 2 * near)) % chips
+
     def send_docs(first, last):
         def body(u, carry):
             for copy in pair_of(u):
@@ -196,33 +217,33 @@
     arrived[0] = out_ref[me]
     counts[0] = cnt_ref[me]
     send_docs(1, group)
-    pieces = [(at, min(at + EARLY, n)) for at in range(group, n, EARLY)]
-
-    for step in range(1, chips):
-        if pieces:
-            send_docs(*pieces.pop(0))
-        low, high = col - 2 * step, col + 2 * step
-
-        @pl.when(place >= step)
-        def _():
-            along(low, col, up_send).wait_recv()
-            across(low).start()
-
-        @pl.when((place >= step) & (place < chips - 1))
-        def _():
-            along(low, col + 2, up_send).start()
-
-        @pl.when(place < chips - step)
-        def _():
-            along(high, col, down_send).wait_recv()
-            across(high).start()
-
-        @pl.when((place < chips - step) & (place > 0))
-        def _():
-            along(high, col - 2, down_send).start()
-
-    if pieces:
-        send_docs(pieces[0][0], n)
+
+    def send_group(k):
+        at = apart(k, upper) * group
+        send_docs(at, at + group)
+
+    for k in range(1, chips - 1):
+        send_group(k)
+
+    @pl.when(place == entry)
+    def _():
+        for i in range(side):
+            source = beyond(i)
+            relay(source, place).wait_recv()
+            across(2 * source + core).start()
+            for j in range(1, side):
+                relay(source, sibling(j)).start()
+
+    send_group(chips - 1)
+    for j in range(1, side):
+        relay(sibling(j), place).wait_recv()
+        across(2 * sibling(j) + core).start()
+
+    @pl.when(place != entry)
+    def _():
+        for i in range(side):
+            relay(beyond(i), place).wait_recv()
+            across(2 * beyond(i) + core).start()
 
     for q in range(chips):
         across(2 * q + 1 - core).wait_recv()
@@ -238,7 +259,7 @@
         lax.fori_loop(first, last, body, 0)
 
     def unpack(k, at):
-        block = arrived[pl.ds(k * group, group)].astype(f32)
+        block = arrived[pl.ds(apart(k, 1 - place % 2) * group, group)].astype(f32)
         if per == kept:
             first, last = block[:, :kept], block[:, lines - kept :]
         else:
@@ -280,10 +301,10 @@
             eb[at, cols] = er.astype(bf16)
             both = both + fold(er * pp)
         both = jnp.sum(both, axis=-1, keepdims=True) * (1.0 / width)
-        mm[at, :] = jnp.broadcast_to(both, (at.size, 128)) * r * r
+        rr[at, :] = jnp.broadcast_to(both, (at.size, 128)) * r * r
 
     def slopes(at, weights, turn):
-        m, rw = mm[at, :], rx[at, :]
+        m, rw = rr[at, :], rx[at, :]
         for n0, nn in blocks:
             cols = pl.ds(n0, nn)
             qq = product(eb[at, :], weights(cols), 1, 1)
@@ -328,7 +349,8 @@
 
         @pl.when(k < chips - 1)
         def _():
-            arrive((k + 1) * group, (k + 2) * group)
+            first = apart(k + 1, 1 - place % 2) * group
+            arrive(first, first + group)
 
         return carry
 
@@ -402,7 +424,7 @@
 
     def sone_copy(k):
         return pltpu.make_async_remote_copy(
-            src_ref=part_buf.at[k],
+            src_ref=one_out.at[2 * ((place + k) % chips) + core],
             dst_ref=one_buf.at[k],
             send_sem=sone_send.at[k],
             recv_sem=sone_recv.at[k],
@@ -416,17 +438,28 @@
     for k in range(1, chips):
         q = (place + k) % chips
         spair_copy(q).wait_recv()
-        part_buf[k] = (one_out[2 * q + core].astype(f32) + pair_buf[q].astype(f32)).astype(bf16)
+        one_out[2 * q + core] = (
+            one_out[2 * q + core].astype(f32) + pair_buf[q].astype(f32)
+        ).astype(bf16)
         sone_copy(k).start()
+    loads[3].wait()
+    loads[4].wait()
     spair_copy(place).wait_recv()
-    share_one[...] = one_out[col].astype(f32) + pair_buf[place].astype(f32)
-    share_two[...] = two_out[row].astype(f32)
+
+    def finish(share, level, moment, new, following):
+        following[...] = momentum_decay * moment[...] + share
+        new[...] = level[...] - outer_rate * (share + momentum_decay * following[...])
+
+    share = two_out[row].astype(f32)
     for k in range(1, n_row):
         stwo_copy(k).wait_recv()
-        share_two[...] += two_buf[k].astype(f32)
+        share = share + two_buf[k].astype(f32)
+    finish(share / n_row, two_v, moment_two, new_two, next_two)
+    share = one_out[col].astype(f32) + pair_buf[place].astype(f32)
     for k in range(1, chips):
         sone_copy(k).wait_recv()
-        share_one[...] += one_buf[k].astype(f32)
+        share = share + one_buf[k].astype(f32)
+    finish(share / n_col, one_v, moment_one, new_one, next_one)
 
     def sent(u, carry):
         for copy in pair_of(u):
@@ -434,18 +467,18 @@
         return carry
 
     lax.fori_loop(1, n, sent, 0)
+    own_copy(other_entry).wait_send()
+    for j in range(1, side):
+        own_copy(sibling(j)).wait_send()
+
+    @pl.when(place == entry)
+    def _():
+        for i in range(side):
+            for j in range(1, side):
+                relay(beyond(i), sibling(j)).wait_send()
+
     for q in range(chips):
-        block = 2 * q + core
-        across(block).wait_send()
-
-        @pl.when((place >= q) & (place < chips - 1))
-        def _():
-            along(block, col + 2, up_send).wait_send()
-
-        @pl.when((place <= q) & (place > 0))
-        def _():
-            along(block, col - 2, down_send).wait_send()
-
+        across(2 * q + core).wait_send()
         spair_copy(q).wait_send()
     for k in range(1, n_row):
         two_copy(k).wait_send()
@@ -472,16 +505,17 @@
     full = pltpu.VMEM((rows, width), f32)
     thin = pltpu.VMEM((rows, width), bf16)
     side = pltpu.VMEM((rows, 128), f32)
-    share_one, share_two = pl.pallas_call(
+    wide_one = jax.ShapeDtypeStruct((one_rows, width), f32)
+    wide_two = jax.ShapeDtypeStruct((two_rows, width), f32)
+    results = pl.pallas_call(
         functools.partial(round_kernel, n_row, n_col, cap, kept),
-        out_shape=(
-            jax.ShapeDtypeStruct((one_rows, width), f32),
-            jax.ShapeDtypeStruct((two_rows, width), f32),
-        ),
-        in_specs=[vmem, hbm, hbm, hbm],
-        out_specs=(vmem,) * 2,
+        out_shape=(wide_one, wide_two, wide_one, wide_two),
+        in_specs=[vmem, hbm, hbm, hbm, hbm, hbm],
+        out_specs=(vmem,) * 4,
         scratch_shapes=[
             pltpu.VMEM((count, length, width), bf16),
+            pltpu.VMEM((one_rows, width), f32),
+            pltpu.VMEM((two_rows, width), f32),
             pltpu.VMEM((one_rows, width), f32),
             pltpu.VMEM((two_rows, width), f32),
             pltpu.VMEM((paths, lines, width), bf16),
@@ -494,15 +528,14 @@
             pltpu.VMEM((rows, rows), bf16),
             pltpu.VMEM((2, width, width), bf16),
             pltpu.VMEM((width, width), f32),
-            side, side, side,
+            side, side,
             pltpu.VMEM((n_col, one_rows, width), bf16),
             pltpu.VMEM((n_row, two_rows, width), bf16),
             pltpu.VMEM((chips, one_rows, width), bf16),
             pltpu.VMEM((chips, one_rows, width), bf16),
-            pltpu.VMEM((chips, one_rows, width), bf16),
             pltpu.VMEM((n_row, two_rows, width), bf16),
-            dma((3,)), dma((paths,)), dma((paths,)), dma((paths,)), dma((paths,)),
-            dma((n_col,)), dma((n_col,)), dma((n_col,)), dma((n_col,)), dma((n_col,)),
+            dma((5,)), dma((paths,)), dma((paths,)), dma((paths,)), dma((paths,)),
+            dma((chips,)), dma((chips, chips)), dma((n_col,)), dma((n_col,)), dma((n_col,)),
             dma((n_row,)), dma((n_row,)),
             dma((chips,)), dma((chips,)), dma((chips,)), dma((chips,)),
             dma((n_row,)), dma((n_row,)),
@@ -510,14 +543,10 @@
         compiler_params=pltpu.CompilerParams(
             collective_id=0, has_side_effects=True, vmem_limit_bytes=67043328
         ),
-    )(routes.reshape(1, count), docs, level_one[0], level_two[0])
-    delta_one = (share_one / n_col)[None]
-    delta_two = (share_two / n_row)[None]
-    next_moment_one = momentum_decay * moment_one + delta_one
-    next_moment_two = momentum_decay * moment_two + delta_two
-    new_one = level_one - outer_rate * (delta_one + momentum_decay * next_moment_one)
-    new_two = level_two - outer_rate * (delta_two + momentum_decay * next_moment_two)
-    return (new_one, new_two, next_moment_one, next_moment_two)
+    )(
+        routes.reshape(1, count), docs, level_one[0], level_two[0], moment_one[0], moment_two[0]
+    )
+    return tuple(result[None] for result in results)
 
 
 def solution(mesh):

time: 112 us -> 106 us (0.946)
  the two profiles are of different devices: /device:TPU:16 before, /device:TPU:0 now
where the time goes in v2:
time: 106 us
  Pallas kernels  100 us (94%)
  local copies, waits for them, and re-layouts  4.72 us (4%)
    pallas_call x1, Pallas kernels, shards(): pl.pallas_call(functools.partial(round_kernel, n_row, n_col, cap, kept),...  100 us
    unnamed x10, local copies, waits for them, and re-layouts  4.72 us

profile of v2, /device:TPU:0, one launch (start us, length us, event | category | flops | bytes accessed | tf_op | source)
XLA Modules:
  0.0 105.7 jit_solution(8680645197438235918)
XLA Ops:
  0.6 100.3 %shard_map.93 = (f32[112,896]{1,0:T(8,128)}, f32[224,896]{1,0:T(8,128)}, f32[112,896]{1,0:T(8,128)}, f32[224,896]{1,0:T(8,128)}) custom-call(s32[1,128]{1,0:T(1,128)} %bitcast.17, bf16[128,4,896]{2,1,0:T(4,128)(2,1)} %docs_hbm.1, f32[112,896]{1,0:T(8,128)} %bitcast.15, f32[224,896]{1,0:T(8,128)} %bitcast.9, f32[112,896]{1,0:T(8,128)} %bitcast.16, ...), custom_call_target="tpu_custom_call" | custom-call | tf_op jit(solution)/shard_map/pallas_call | solution.py:510
  100.9 0.0 copy-start.1
  101.0 1.8 %copy.14 = f32[1,112,896]{2,1,0:T(8,128)} copy(f32[1,112,896]{2,1,0:T(8,128)} %bitcast.14) | data formatting | bytes 802816
  102.8 0.0 copy-done.1
  102.8 0.0 copy-start.2
  102.8 0.0 copy-start
  102.8 0.9 copy.15
  103.7 0.3 copy-done.2
  104.0 0.7 copy.16
  104.8 0.0 copy-done
  104.8 0.9 copy.17
Async XLA Ops:
  100.9 1.9 %copy-start.1 = (f32[224,896]{1,0:T(8,128)S(1)}, f32[224,896]{1,0:T(8,128)}, u32[]{:S(2)}) copy-start(f32[224,896]{1,0:T(8,128)} %get-tuple-element.9) | copy-start | bytes 2408452
  102.8 1.2 %copy-start.2 = (f32[112,896]{1,0:T(8,128)S(1)}, f32[112,896]{1,0:T(8,128)}, u32[]{:S(2)}) copy-start(f32[112,896]{1,0:T(8,128)} %get-tuple-element.10) | copy-start | bytes 1204228
  102.8 2.0 %copy-start = (f32[224,896]{1,0:T(8,128)S(1)}, f32[224,896]{1,0:T(8,128)}, u32[]{:S(2)}) copy-start(f32[224,896]{1,0:T(8,128)} %get-tuple-element.11) | copy-start | bytes 2408452

commit v3 on v2

--- a/solution.py
+++ b/solution.py
@@ -1,4 +1,5 @@
 import functools
+import math
 
 import jax
 import jax.numpy as jnp
@@ -41,10 +42,10 @@
     new_one, new_two, next_one, next_two,
     docs_v, one_v, two_v, moment_one, moment_two, out_ref, cnt_ref, arrived, counts, whole_one, whole_two,
     z, h, g, e, ds, t, xb, hb, eb, db, gram, w2, dw, rx, rr,
-    one_out, two_out, pair_buf, one_buf, two_buf,
+    one_out, two_out, pair_buf, pre_buf, one_buf, two_buf,
     load_sem, doc_send, doc_recv, cnt_send, cnt_recv,
     own_send, relay_send, one_recv, pair_send, pair_recv, two_send, two_recv,
-    spair_send, spair_recv, sone_send, sone_recv, stwo_send, stwo_recv,
+    spair_send, spair_recv, pre_send, pre_recv, sone_send, sone_recv, stwo_send, stwo_recv, out_sem,
 ):
     row, col = lax.axis_index("row"), lax.axis_index("col")
     n = n_row * n_col
@@ -62,7 +63,7 @@
     per = rows // n
     group = 2 * n_row
     chunk = group * per
-    half = rows // 2
+    early = rows * (chips - 1) // chips // 256 * 256
     count = docs_v.shape[0]
     length = docs_v.shape[1]
     scale = width ** (-0.5)
@@ -91,6 +92,73 @@
     whole_one[col] = one_v[...].astype(bf16)
     loads[1].wait()
     whole_two[row] = two_v[...].astype(bf16)
+
+    pl.semaphore_wait(barrier, n - 1)
+
+    def own_copy(to):
+        return pltpu.make_async_remote_copy(
+            src_ref=whole_one.at[col],
+            dst_ref=whole_one.at[col],
+            send_sem=own_send.at[to],
+            recv_sem=one_recv.at[col],
+            device_id={"row": row, "col": 2 * to + core},
+            device_id_type=MESH,
+        )
+
+    def relay(source, to):
+        block = 2 * source + core
+        return pltpu.make_async_remote_copy(
+            src_ref=whole_one.at[block],
+            dst_ref=whole_one.at[block],
+            send_sem=relay_send.at[source, to],
+            recv_sem=one_recv.at[block],
+            device_id={"row": row, "col": 2 * to + core},
+            device_id_type=MESH,
+        )
+
+    def sibling(j):
+        return base + (place - base + j) % side
+
+    def beyond(i):
+        return (1 - upper) * (side + i) + upper * (side - 1 - i)
+
+    def across(block):
+        return pltpu.make_async_remote_copy(
+            src_ref=whole_one.at[block],
+            dst_ref=whole_one.at[block],
+            send_sem=pair_send.at[block],
+            recv_sem=pair_recv.at[block],
+            device_id={"row": row, "col": partner},
+            device_id_type=MESH,
+        )
+
+    def two_copy(k):
+        return pltpu.make_async_remote_copy(
+            src_ref=whole_two.at[row],
+            dst_ref=whole_two.at[row],
+            send_sem=two_send.at[k],
+            recv_sem=two_recv.at[k],
+            device_id={"row": (row + k) % n_row, "col": col},
+            device_id_type=MESH,
+        )
+
+    def two_wait(k):
+        from_row = (row - k + n_row) % n_row
+        return pltpu.make_async_remote_copy(
+            src_ref=whole_two.at[row],
+            dst_ref=whole_two.at[from_row],
+            send_sem=two_send.at[k],
+            recv_sem=two_recv.at[k],
+            device_id={"row": (row + k) % n_row, "col": col},
+            device_id_type=MESH,
+        )
+
+    own_copy(other_entry).start()
+    for j in range(1, side):
+        own_copy(sibling(j)).start()
+    across(col).start()
+    for k in range(1, n_row):
+        two_copy(k).start()
 
     target = route_ref[...]
     named = jnp.broadcast_to(target.astype(f32), (count, count))
@@ -104,73 +172,6 @@
     path = lax.broadcasted_iota(jnp.int32, (n, 1, count), 0)
     mine = jnp.where(jnp.broadcast_to(target[None], (n, 1, count)) == path, 1.0, 0.0)
     cnt_ref[...] = jnp.broadcast_to(jnp.sum(mine, axis=-1, keepdims=True), cnt_ref.shape)
-
-    pl.semaphore_wait(barrier, n - 1)
-
-    def own_copy(to):
-        return pltpu.make_async_remote_copy(
-            src_ref=whole_one.at[col],
-            dst_ref=whole_one.at[col],
-            send_sem=own_send.at[to],
-            recv_sem=one_recv.at[col],
-            device_id={"row": row, "col": 2 * to + core},
-            device_id_type=MESH,
-        )
-
-    def relay(source, to):
-        block = 2 * source + core
-        return pltpu.make_async_remote_copy(
-            src_ref=whole_one.at[block],
-            dst_ref=whole_one.at[block],
-            send_sem=relay_send.at[source, to],
-            recv_sem=one_recv.at[block],
-            device_id={"row": row, "col": 2 * to + core},
-            device_id_type=MESH,
-        )
-
-    def sibling(j):
-        return base + (place - base + j) % side
-
-    def beyond(i):
-        return (1 - upper) * (side + i) + upper * (side - 1 - i)
-
-    def across(block):
-        return pltpu.make_async_remote_copy(
-            src_ref=whole_one.at[block],
-            dst_ref=whole_one.at[block],
-            send_sem=pair_send.at[block],
-            recv_sem=pair_recv.at[block],
-            device_id={"row": row, "col": partner},
-            device_id_type=MESH,
-        )
-
-    def two_copy(k):
-        return pltpu.make_async_remote_copy(
-            src_ref=whole_two.at[row],
-            dst_ref=whole_two.at[row],
-            send_sem=two_send.at[k],
-            recv_sem=two_recv.at[k],
-            device_id={"row": (row + k) % n_row, "col": col},
-            device_id_type=MESH,
-        )
-
-    def two_wait(k):
-        from_row = (row - k + n_row) % n_row
-        return pltpu.make_async_remote_copy(
-            src_ref=whole_two.at[row],
-            dst_ref=whole_two.at[from_row],
-            send_sem=two_send.at[k],
-            recv_sem=two_recv.at[k],
-            device_id={"row": (row + k) % n_row, "col": col},
-            device_id_type=MESH,
-        )
-
-    own_copy(other_entry).start()
-    for j in range(1, side):
-        own_copy(sibling(j)).start()
-    across(col).start()
-    for k in range(1, n_row):
-        two_copy(k).start()
 
     loads[2].wait()
     docs = jnp.swapaxes(docs_v[...], 0, 1)
@@ -326,7 +327,7 @@
         return whole_two[...].reshape(width, width)[cols.start : cols.start + cols.size]
 
     arrive(1, group)
-    low, high = pl.ds(0, half), pl.ds(half, half)
+    low, high = pl.ds(0, early), pl.ds(early, rows - early)
 
     def first_turn(k, carry):
         at = pl.ds(pl.multiple_of(k * chunk, chunk), chunk)
@@ -340,7 +341,7 @@
         errors(at, two_cols)
         slopes(at, two_rows, None)
 
-        @pl.when(k == chips // 2 - 1)
+        @pl.when(k == chips - 2)
         def _():
             gram[low, low] = product(xb[low, :], xb[low, :], 1, 1).astype(bf16)
             for n0, nn in blocks:
@@ -422,44 +423,118 @@
             device_id_type=MESH,
         )
 
-    def sone_copy(k):
-        return pltpu.make_async_remote_copy(
-            src_ref=one_out.at[2 * ((place + k) % chips) + core],
-            dst_ref=one_buf.at[k],
-            send_sem=sone_send.at[k],
-            recv_sem=sone_recv.at[k],
-            device_id={"row": row, "col": (col + 2 * k) % n_col},
-            device_id_type=MESH,
-        )
-
-    for k in range(1, chips):
-        spair_copy((place + k) % chips).start()
+    inner = (place == entry).astype(jnp.int32)
+    other = side - base
+
+    def far(i):
+        return other + (other_entry - other + i + inner) % side
+
+    def sone_copy(to):
+        return pltpu.make_async_remote_copy(
+            src_ref=one_out.at[2 * to + core],
+            dst_ref=one_buf.at[place],
+            send_sem=sone_send.at[to],
+            recv_sem=sone_recv.at[place],
+            device_id={"row": row, "col": 2 * to + core},
+            device_id_type=MESH,
+        )
+
+    def sone_from(source):
+        return pltpu.make_async_remote_copy(
+            src_ref=one_out.at[2 * source + core],
+            dst_ref=one_buf.at[source],
+            send_sem=sone_send.at[source],
+            recv_sem=sone_recv.at[source],
+            device_id={"row": row, "col": 2 * source + core},
+            device_id_type=MESH,
+        )
+
+    def pre_copy(source):
+        return pltpu.make_async_remote_copy(
+            src_ref=one_out.at[2 * other_entry + core],
+            dst_ref=pre_buf.at[source - base],
+            send_sem=pre_send.at[0],
+            recv_sem=pre_recv.at[source - base],
+            device_id={"row": row, "col": 2 * entry + core},
+            device_id_type=MESH,
+        )
+
+    wanted = [far(i) for i in range(side)] + [sibling(j) for j in range(1, side)]
+    for q in wanted:
+        spair_copy(q).start()
     spair_copy(place).start()
-    for k in range(1, chips):
-        q = (place + k) % chips
+    for i, q in enumerate(wanted):
         spair_copy(q).wait_recv()
         one_out[2 * q + core] = (
             one_out[2 * q + core].astype(f32) + pair_buf[q].astype(f32)
         ).astype(bf16)
-        sone_copy(k).start()
+        if i in (0, side - 1):
+            first = 1 if i == 0 else 0
+
+            @pl.when(inner == first)
+            def _():
+                sone_copy(q).start()
+
+            if i == 0:
+
+                @pl.when(inner == 0)
+                def _():
+                    pre_copy(place).start()
+
+        else:
+            sone_copy(q).start()
+
+    @pl.when(inner == 1)
+    def _():
+        share = one_out[2 * other_entry + core].astype(f32)
+        for j in range(1, side):
+            pre_copy(sibling(j)).wait_recv()
+            share = share + pre_buf[sibling(j) - base].astype(f32)
+        one_out[2 * other_entry + core] = share.astype(bf16)
+        sone_copy(other_entry).start()
+
     loads[3].wait()
     loads[4].wait()
-    spair_copy(place).wait_recv()
-
-    def finish(share, level, moment, new, following):
-        following[...] = momentum_decay * moment[...] + share
-        new[...] = level[...] - outer_rate * (share + momentum_decay * following[...])
-
+
+    def finish(share, level, moment):
+        following = momentum_decay * moment[...] + share
+        moment[...] = following
+        level[...] = level[...] - outer_rate * (share + momentum_decay * following)
+
+    stores = [
+        pltpu.make_async_copy(one_v, new_one, out_sem.at[0]),
+        pltpu.make_async_copy(two_v, new_two, out_sem.at[1]),
+        pltpu.make_async_copy(moment_one, next_one, out_sem.at[2]),
+        pltpu.make_async_copy(moment_two, next_two, out_sem.at[3]),
+    ]
     share = two_out[row].astype(f32)
     for k in range(1, n_row):
         stwo_copy(k).wait_recv()
         share = share + two_buf[k].astype(f32)
-    finish(share / n_row, two_v, moment_two, new_two, next_two)
-    share = one_out[col].astype(f32) + pair_buf[place].astype(f32)
-    for k in range(1, chips):
-        sone_copy(k).wait_recv()
-        share = share + one_buf[k].astype(f32)
-    finish(share / n_col, one_v, moment_one, new_one, next_one)
+    finish(share / n_row, two_v, moment_two)
+    stores[1].start()
+    stores[3].start()
+    spair_copy(place).wait_recv()
+    total = ds.at[pl.ds(0, width // n_col), :]
+    total[...] = one_out[col].astype(f32) + pair_buf[place].astype(f32)
+    for j in range(1, side):
+        sone_from(sibling(j)).wait_recv()
+        total[...] += one_buf[sibling(j)].astype(f32)
+
+    @pl.when(inner == 1)
+    def _():
+        sone_from(other_entry).wait_recv()
+        total[...] += one_buf[other_entry].astype(f32)
+
+    @pl.when(inner == 0)
+    def _():
+        for i in range(side):
+            sone_from(far(i)).wait_recv()
+            total[...] += one_buf[far(i)].astype(f32)
+
+    finish(total[...] / n_col, one_v, moment_one)
+    stores[0].start()
+    stores[2].start()
 
     def sent(u, carry):
         for copy in pair_of(u):
@@ -483,8 +558,37 @@
     for k in range(1, n_row):
         two_copy(k).wait_send()
         stwo_copy(k).wait_send()
-    for k in range(1, chips):
-        sone_copy(k).wait_send()
+    for j in range(1, side):
+        sone_copy(sibling(j)).wait_send()
+    for i in range(1, side - 1):
+        sone_copy(far(i)).wait_send()
+
+    @pl.when(inner == 1)
+    def _():
+        for i in sorted({0, side - 1}):
+            sone_copy(far(i)).wait_send()
+
+    @pl.when(inner == 0)
+    def _():
+        sone_copy(far(side - 1)).wait_send()
+        pre_copy(place).wait_send()
+
+    for store in stores:
+        store.wait()
+
+
+def pass_kernel(*refs):
+    sources, results, held = refs[:4], refs[4:8], refs[8:12]
+    in_sem, out_sem = refs[12:]
+    arriving = [pltpu.make_async_copy(sources[i], held[i], in_sem.at[i]) for i in range(4)]
+    leaving = [pltpu.make_async_copy(held[i], results[i], out_sem.at[i]) for i in range(4)]
+    for copy in arriving:
+        copy.start()
+    for i in range(4):
+        arriving[i].wait()
+        leaving[i].start()
+    for copy in leaving:
+        copy.wait()
 
 
 def shards(docs, routes, level_one, level_two, moment_one, moment_two):
@@ -505,47 +609,65 @@
     full = pltpu.VMEM((rows, width), f32)
     thin = pltpu.VMEM((rows, width), bf16)
     side = pltpu.VMEM((rows, 128), f32)
+    scratch = [
+        pltpu.VMEM((count, length, width), bf16),
+        pltpu.VMEM((one_rows, width), f32),
+        pltpu.VMEM((two_rows, width), f32),
+        pltpu.VMEM((one_rows, width), f32),
+        pltpu.VMEM((two_rows, width), f32),
+        pltpu.VMEM((paths, lines, width), bf16),
+        pltpu.VMEM((paths, 1, 128), f32),
+        pltpu.VMEM((paths, lines, width), bf16),
+        pltpu.VMEM((paths, 1, 128), f32),
+        pltpu.VMEM((n_col, one_rows, width), bf16),
+        pltpu.VMEM((n_row, two_rows, width), bf16),
+        full, full, full, full, full, thin, thin, thin, thin, thin,
+        pltpu.VMEM((rows, rows), bf16),
+        pltpu.VMEM((2, width, width), bf16),
+        pltpu.VMEM((width, width), f32),
+        side, side,
+        pltpu.VMEM((n_col, one_rows, width), bf16),
+        pltpu.VMEM((n_row, two_rows, width), bf16),
+        pltpu.VMEM((chips, one_rows, width), bf16),
+        pltpu.VMEM((chips // 2, one_rows, width), bf16),
+        pltpu.VMEM((chips, one_rows, width), bf16),
+        pltpu.VMEM((n_row, two_rows, width), bf16),
+        dma((5,)), dma((paths,)), dma((paths,)), dma((paths,)), dma((paths,)),
+        dma((chips,)), dma((chips, chips)), dma((n_col,)), dma((n_col,)), dma((n_col,)),
+        dma((n_row,)), dma((n_row,)),
+        dma((chips,)), dma((chips,)), dma((1,)), dma((chips // 2,)), dma((chips,)), dma((chips,)),
+        dma((n_row,)), dma((n_row,)), dma((4,)),
+    ]
+    held = sum(
+        math.prod(piece.shape) * piece.dtype.itemsize
+        for piece in scratch
+        if piece.memory_space == pltpu.VMEM
+    )
+    limit = min(67043328, held + (12 << 20))
     wide_one = jax.ShapeDtypeStruct((one_rows, width), f32)
     wide_two = jax.ShapeDtypeStruct((two_rows, width), f32)
     results = pl.pallas_call(
         functools.partial(round_kernel, n_row, n_col, cap, kept),
         out_shape=(wide_one, wide_two, wide_one, wide_two),
         in_specs=[vmem, hbm, hbm, hbm, hbm, hbm],
-        out_specs=(vmem,) * 4,
-        scratch_shapes=[
-            pltpu.VMEM((count, length, width), bf16),
-            pltpu.VMEM((one_rows, width), f32),
-            pltpu.VMEM((two_rows, width), f32),
-            pltpu.VMEM((one_rows, width), f32),
-            pltpu.VMEM((two_rows, width), f32),
-            pltpu.VMEM((paths, lines, width), bf16),
-            pltpu.VMEM((paths, 1, 128), f32),
-            pltpu.VMEM((paths, lines, width), bf16),
-            pltpu.VMEM((paths, 1, 128), f32),
-            pltpu.VMEM((n_col, one_rows, width), bf16),
-            pltpu.VMEM((n_row, two_rows, width), bf16),
-            full, full, full, full, full, thin, thin, thin, thin, thin,
-            pltpu.VMEM((rows, rows), bf16),
-            pltpu.VMEM((2, width, width), bf16),
-            pltpu.VMEM((width, width), f32),
-            side, side,
-            pltpu.VMEM((n_col, one_rows, width), bf16),
-            pltpu.VMEM((n_row, two_rows, width), bf16),
-            pltpu.VMEM((chips, one_rows, width), bf16),
-            pltpu.VMEM((chips, one_rows, width), bf16),
-            pltpu.VMEM((n_row, two_rows, width), bf16),
-            dma((5,)), dma((paths,)), dma((paths,)), dma((paths,)), dma((paths,)),
-            dma((chips,)), dma((chips, chips)), dma((n_col,)), dma((n_col,)), dma((n_col,)),
-            dma((n_row,)), dma((n_row,)),
-            dma((chips,)), dma((chips,)), dma((chips,)), dma((chips,)),
-            dma((n_row,)), dma((n_row,)),
-        ],
+        out_specs=(hbm,) * 4,
+        scratch_shapes=scratch,
         compiler_params=pltpu.CompilerParams(
-            collective_id=0, has_side_effects=True, vmem_limit_bytes=67043328
+            collective_id=0, has_side_effects=True, vmem_limit_bytes=limit
         ),
     )(
         routes.reshape(1, count), docs, level_one[0], level_two[0], moment_one[0], moment_two[0]
     )
+    results = pl.pallas_call(
+        pass_kernel,
+        out_shape=(wide_one, wide_two, wide_one, wide_two),
+        in_specs=[hbm] * 4,
+        out_specs=(hbm,) * 4,
+        scratch_shapes=[
+            pltpu.VMEM(piece.shape, piece.dtype) for piece in (wide_one, wide_two, wide_one, wide_two)
+        ]
+        + [dma((4,)), dma((4,))],
+    )(*results)
     return tuple(result[None] for result in results)
 
 

time: 106 us -> 104 us (0.981)
  local copies, waits for them, and re-layouts: 4.72 us -> 0 us
  Pallas kernels: 100 us -> 103 us
    unnamed x10 -> x0, local copies, waits for them, and re-layouts: 4.72 us -> none
    pallas_call x0 -> x1, Pallas kernels: none -> 2.62 us  [shards(): pl.pallas_call(pass_kernel, out_shape=(wide_one, wide_two, wide_one, wide...]
where the time goes in v3:
time: 104 us
  Pallas kernels  103 us (99%)
    pallas_call x1, Pallas kernels, shards(): pl.pallas_call(functools.partial(round_kernel, n_row, n_col, cap, kept),...  101 us
    pallas_call x1, Pallas kernels, shards(): pl.pallas_call(pass_kernel, out_shape=(wide_one, wide_two, wide_one, wide...  2.62 us

profile of v3, /device:TPU:0, one launch (start us, length us, event | category | flops | bytes accessed | tf_op | source)
XLA Modules:
  0.0 104.0 jit_solution(16332279402758272725)
XLA Ops:
  0.6 100.6 %shard_map.93 = (f32[112,896]{1,0:T(8,128)}, f32[224,896]{1,0:T(8,128)}, f32[112,896]{1,0:T(8,128)}, f32[224,896]{1,0:T(8,128)}) custom-call(s32[1,128]{1,0:T(1,128)} %bitcast.13, bf16[128,4,896]{2,1,0:T(4,128)(2,1)} %docs_hbm.1, f32[112,896]{1,0:T(8,128)} %bitcast.11, f32[224,896]{1,0:T(8,128)} %bitcast.9, f32[112,896]{1,0:T(8,128)} %bitcast.12, ...), custom_call_target="tpu_custom_call" | custom-call | tf_op jit(solution)/shard_map/pallas_call | solution.py:649
  101.2 2.6 %shard_map.94 = (f32[112,896]{1,0:T(8,128)}, f32[224,896]{1,0:T(8,128)}, f32[112,896]{1,0:T(8,128)}, f32[224,896]{1,0:T(8,128)}) custom-call(f32[112,896]{1,0:T(8,128)} %get-tuple-element.12.refs_0_, f32[224,896]{1,0:T(8,128)} %get-tuple-element.13.refs_1_, f32[112,896]{1,0:T(8,128)} %get-tuple-element.14.refs_2_, f32[224,896]{1,0:T(8,128)} %get-tuple-element.15.refs_3_), custom_call_target="tpu_custom_call" | custom-call | tf_op jit(solution)/shard_map/pallas_call | solution.py:661

commit v4 on v3

--- a/solution.py
+++ b/solution.py
@@ -57,12 +57,16 @@
     upper = place // side
     base = upper * side
     entry = side - 1 + upper
+    inner = (place == entry).astype(jnp.int32)
+    outer = 1 - inner
     other_entry = side - upper
     lines, width = arrived.shape[1:]
     rows = z.shape[0]
     per = rows // n
     group = 2 * n_row
-    chunk = group * per
+    half_group = group // 2
+    chunk = half_group * per
+    chunks = 2 * chips
     early = rows * (chips - 1) // chips // 256 * 256
     count = docs_v.shape[0]
     length = docs_v.shape[1]
@@ -203,8 +207,8 @@
             ),
         )
 
-    def apart(k, flip):
-        near = k * 2 % chips + k // (chips // 2)
+    def apart(k, mixed, flip):
+        near = k + mixed * (k * 2 % chips + k // (chips // 2) - k)
         return (near + flip * (chips - 2 * near)) % chips
 
     def send_docs(first, last):
@@ -220,7 +224,7 @@
     send_docs(1, group)
 
     def send_group(k):
-        at = apart(k, upper) * group
+        at = apart(k, inner, upper) * group
         send_docs(at, at + group)
 
     for k in range(1, chips - 1):
@@ -251,6 +255,10 @@
     for k in range(1, n_row):
         two_wait(k).wait_recv()
 
+    def place_of(k):
+        flip = upper * inner + (1 - upper) * outer
+        return apart(k // 2, outer, flip) * group + k % 2 * half_group
+
     def arrive(first, last):
         def body(u, carry):
             for copy in pair_of(u):
@@ -260,7 +268,7 @@
         lax.fori_loop(first, last, body, 0)
 
     def unpack(k, at):
-        block = arrived[pl.ds(apart(k, 1 - place % 2) * group, group)].astype(f32)
+        block = arrived[pl.ds(place_of(k), half_group)].astype(f32)
         if per == kept:
             first, last = block[:, :kept], block[:, lines - kept :]
         else:
@@ -326,7 +334,7 @@
     def two_rows(cols):
         return whole_two[...].reshape(width, width)[cols.start : cols.start + cols.size]
 
-    arrive(1, group)
+    arrive(1, half_group)
     low, high = pl.ds(0, early), pl.ds(early, rows - early)
 
     def first_turn(k, carry):
@@ -341,21 +349,21 @@
         errors(at, two_cols)
         slopes(at, two_rows, None)
 
-        @pl.when(k == chips - 2)
+        @pl.when(k == chunks - 3)
         def _():
             gram[low, low] = product(xb[low, :], xb[low, :], 1, 1).astype(bf16)
             for n0, nn in blocks:
                 cols = pl.ds(n0, nn)
                 dw[:, cols] = product(hb[low, :], eb[low, cols], 0, 0)
 
-        @pl.when(k < chips - 1)
+        @pl.when(k < chunks - 1)
         def _():
-            first = apart(k + 1, 1 - place % 2) * group
-            arrive(first, first + group)
+            first = place_of(k + 1)
+            arrive(first, first + half_group)
 
         return carry
 
-    lax.fori_loop(0, chips, first_turn, 0)
+    lax.fori_loop(0, chunks, first_turn, 0)
     gram[high, :] = product(xb[high, :], xb[...], 1, 1).astype(bf16)
     gram[low, high] = product(xb[low, :], xb[high, :], 1, 1).astype(bf16)
 
@@ -423,7 +431,6 @@
             device_id_type=MESH,
         )
 
-    inner = (place == entry).astype(jnp.int32)
     other = side - base
 
     def far(i):

time: 104 us -> 103 us (level)
  no operation moved by 1% of the time
where the time goes in v4:
time: 103 us
  Pallas kernels  102 us (99%)
    pallas_call x1, Pallas kernels, shards(): pl.pallas_call(functools.partial(round_kernel, n_row, n_col, cap, kept),...  99.8 us
    pallas_call x1, Pallas kernels, shards(): pl.pallas_call(pass_kernel, out_shape=(wide_one, wide_two, wide_one, wide...  2.62 us

profile of v4, /device:TPU:0, one launch (start us, length us, event | category | flops | bytes accessed | tf_op | source)
XLA Modules:
  0.0 103.2 jit_solution(11603685748920389553)
XLA Ops:
  0.6 99.8 %shard_map.93 = (f32[112,896]{1,0:T(8,128)}, f32[224,896]{1,0:T(8,128)}, f32[112,896]{1,0:T(8,128)}, f32[224,896]{1,0:T(8,128)}) custom-call(s32[1,128]{1,0:T(1,128)} %bitcast.13, bf16[128,4,896]{2,1,0:T(4,128)(2,1)} %docs_hbm.1, f32[112,896]{1,0:T(8,128)} %bitcast.11, f32[224,896]{1,0:T(8,128)} %bitcast.9, f32[112,896]{1,0:T(8,128)} %bitcast.12, ...), custom_call_target="tpu_custom_call" | custom-call | tf_op jit(solution)/shard_map/pallas_call | solution.py:656
  100.4 2.6 %shard_map.94 = (f32[112,896]{1,0:T(8,128)}, f32[224,896]{1,0:T(8,128)}, f32[112,896]{1,0:T(8,128)}, f32[224,896]{1,0:T(8,128)}) custom-call(f32[112,896]{1,0:T(8,128)} %get-tuple-element.12.refs_0_, f32[224,896]{1,0:T(8,128)} %get-tuple-element.13.refs_1_, f32[112,896]{1,0:T(8,128)} %get-tuple-element.14.refs_2_, f32[224,896]{1,0:T(8,128)} %get-tuple-element.15.refs_3_), custom_call_target="tpu_custom_call" | custom-call | tf_op jit(solution)/shard_map/pallas_call | solution.py:668

commit v5 on v4

--- a/solution.py
+++ b/solution.py
@@ -40,12 +40,12 @@
     n_row, n_col, cap, kept,
     route_ref, docs_hbm, one_hbm, two_hbm, moment_one_hbm, moment_two_hbm,
     new_one, new_two, next_one, next_two,
-    docs_v, one_v, two_v, moment_one, moment_two, out_ref, cnt_ref, arrived, counts, whole_one, whole_two,
+    docs_v, out_ref, cnt_ref, arrived, counts, whole_one, whole_two,
     z, h, g, e, ds, t, xb, hb, eb, db, gram, w2, dw, rx, rr,
     one_out, two_out, pair_buf, pre_buf, one_buf, two_buf,
     load_sem, doc_send, doc_recv, cnt_send, cnt_recv,
     own_send, relay_send, one_recv, pair_send, pair_recv, two_send, two_recv,
-    spair_send, spair_recv, pre_send, pre_recv, sone_send, sone_recv, stwo_send, stwo_recv, out_sem,
+    spair_send, spair_recv, pre_send, pre_recv, sone_send, sone_recv, stwo_send, stwo_recv,
 ):
     row, col = lax.axis_index("row"), lax.axis_index("col")
     n = n_row * n_col
@@ -75,11 +75,11 @@
     barrier = pltpu.get_barrier_semaphore()
 
     loads = [
-        pltpu.make_async_copy(one_hbm, one_v, load_sem.at[0]),
-        pltpu.make_async_copy(two_hbm, two_v, load_sem.at[1]),
+        pltpu.make_async_copy(one_hbm, new_one, load_sem.at[0]),
+        pltpu.make_async_copy(two_hbm, new_two, load_sem.at[1]),
         pltpu.make_async_copy(docs_hbm, docs_v, load_sem.at[2]),
-        pltpu.make_async_copy(moment_one_hbm, moment_one, load_sem.at[3]),
-        pltpu.make_async_copy(moment_two_hbm, moment_two, load_sem.at[4]),
+        pltpu.make_async_copy(moment_one_hbm, next_one, load_sem.at[3]),
+        pltpu.make_async_copy(moment_two_hbm, next_two, load_sem.at[4]),
     ]
     for copy in loads:
         copy.start()
@@ -93,9 +93,9 @@
 
     lax.fori_loop(1, n, greet, 0)
     loads[0].wait()
-    whole_one[col] = one_v[...].astype(bf16)
+    whole_one[col] = new_one[...].astype(bf16)
     loads[1].wait()
-    whole_two[row] = two_v[...].astype(bf16)
+    whole_two[row] = new_two[...].astype(bf16)
 
     pl.semaphore_wait(barrier, n - 1)
 
@@ -207,9 +207,8 @@
             ),
         )
 
-    def apart(k, mixed, flip):
-        near = k + mixed * (k * 2 % chips + k // (chips // 2) - k)
-        return (near + flip * (chips - 2 * near)) % chips
+    def apart(k, flip):
+        return (k + flip * (chips - 2 * k)) % chips
 
     def send_docs(first, last):
         def body(u, carry):
@@ -223,12 +222,11 @@
     counts[0] = cnt_ref[me]
     send_docs(1, group)
 
-    def send_group(k):
-        at = apart(k, inner, upper) * group
+    for k in range(1, chips - 1):
+        at = apart(k, upper) * group
         send_docs(at, at + group)
-
-    for k in range(1, chips - 1):
-        send_group(k)
+    at = apart(chips - 1, upper) * group
+    send_docs(at, at + half_group)
 
     @pl.when(place == entry)
     def _():
@@ -239,7 +237,7 @@
             for j in range(1, side):
                 relay(source, sibling(j)).start()
 
-    send_group(chips - 1)
+    send_docs(at + half_group, at + group)
     for j in range(1, side):
         relay(sibling(j), place).wait_recv()
         across(2 * sibling(j) + core).start()
@@ -257,7 +255,7 @@
 
     def place_of(k):
         flip = upper * inner + (1 - upper) * outer
-        return apart(k // 2, outer, flip) * group + k % 2 * half_group
+        return apart(k // 2, flip) * group + k % 2 * half_group
 
     def arrive(first, last):
         def body(u, carry):
@@ -508,19 +506,11 @@
         moment[...] = following
         level[...] = level[...] - outer_rate * (share + momentum_decay * following)
 
-    stores = [
-        pltpu.make_async_copy(one_v, new_one, out_sem.at[0]),
-        pltpu.make_async_copy(two_v, new_two, out_sem.at[1]),
-        pltpu.make_async_copy(moment_one, next_one, out_sem.at[2]),
-        pltpu.make_async_copy(moment_two, next_two, out_sem.at[3]),
-    ]
     share = two_out[row].astype(f32)
     for k in range(1, n_row):
         stwo_copy(k).wait_recv()
         share = share + two_buf[k].astype(f32)
-    finish(share / n_row, two_v, moment_two)
-    stores[1].start()
-    stores[3].start()
+    finish(share / n_row, new_two, next_two)
     spair_copy(place).wait_recv()
     total = ds.at[pl.ds(0, width // n_col), :]
     total[...] = one_out[col].astype(f32) + pair_buf[place].astype(f32)
@@ -539,9 +529,7 @@
             sone_from(far(i)).wait_recv()
             total[...] += one_buf[far(i)].astype(f32)
 
-    finish(total[...] / n_col, one_v, moment_one)
-    stores[0].start()
-    stores[2].start()
+    finish(total[...] / n_col, new_one, next_one)
 
     def sent(u, carry):
         for copy in pair_of(u):
@@ -579,23 +567,6 @@
     def _():
         sone_copy(far(side - 1)).wait_send()
         pre_copy(place).wait_send()
-
-    for store in stores:
-        store.wait()
-
-
-def pass_kernel(*refs):
-    sources, results, held = refs[:4], refs[4:8], refs[8:12]
-    in_sem, out_sem = refs[12:]
-    arriving = [pltpu.make_async_copy(sources[i], held[i], in_sem.at[i]) for i in range(4)]
-    leaving = [pltpu.make_async_copy(held[i], results[i], out_sem.at[i]) for i in range(4)]
-    for copy in arriving:
-        copy.start()
-    for i in range(4):
-        arriving[i].wait()
-        leaving[i].start()
-    for copy in leaving:
-        copy.wait()
 
 
 def shards(docs, routes, level_one, level_two, moment_one, moment_two):
@@ -618,10 +589,6 @@
     side = pltpu.VMEM((rows, 128), f32)
     scratch = [
         pltpu.VMEM((count, length, width), bf16),
-        pltpu.VMEM((one_rows, width), f32),
-        pltpu.VMEM((two_rows, width), f32),
-        pltpu.VMEM((one_rows, width), f32),
-        pltpu.VMEM((two_rows, width), f32),
         pltpu.VMEM((paths, lines, width), bf16),
         pltpu.VMEM((paths, 1, 128), f32),
         pltpu.VMEM((paths, lines, width), bf16),
@@ -643,21 +610,22 @@
         dma((chips,)), dma((chips, chips)), dma((n_col,)), dma((n_col,)), dma((n_col,)),
         dma((n_row,)), dma((n_row,)),
         dma((chips,)), dma((chips,)), dma((1,)), dma((chips // 2,)), dma((chips,)), dma((chips,)),
-        dma((n_row,)), dma((n_row,)), dma((4,)),
+        dma((n_row,)), dma((n_row,)),
     ]
     held = sum(
         math.prod(piece.shape) * piece.dtype.itemsize
         for piece in scratch
         if piece.memory_space == pltpu.VMEM
     )
-    limit = min(67043328, held + (12 << 20))
-    wide_one = jax.ShapeDtypeStruct((one_rows, width), f32)
-    wide_two = jax.ShapeDtypeStruct((two_rows, width), f32)
+    kept_bytes = 8 * (one_rows + two_rows) * width
+    limit = min(67043328 - kept_bytes, held + (12 << 20))
+    held_one = pltpu.VMEM((one_rows, width), f32)
+    held_two = pltpu.VMEM((two_rows, width), f32)
     results = pl.pallas_call(
         functools.partial(round_kernel, n_row, n_col, cap, kept),
-        out_shape=(wide_one, wide_two, wide_one, wide_two),
+        out_shape=(held_one, held_two, held_one, held_two),
         in_specs=[vmem, hbm, hbm, hbm, hbm, hbm],
-        out_specs=(hbm,) * 4,
+        out_specs=(vmem,) * 4,
         scratch_shapes=scratch,
         compiler_params=pltpu.CompilerParams(
             collective_id=0, has_side_effects=True, vmem_limit_bytes=limit
@@ -665,16 +633,6 @@
     )(
         routes.reshape(1, count), docs, level_one[0], level_two[0], moment_one[0], moment_two[0]
     )
-    results = pl.pallas_call(
-        pass_kernel,
-        out_shape=(wide_one, wide_two, wide_one, wide_two),
-        in_specs=[hbm] * 4,
-        out_specs=(hbm,) * 4,
-        scratch_shapes=[
-            pltpu.VMEM(piece.shape, piece.dtype) for piece in (wide_one, wide_two, wide_one, wide_two)
-        ]
-        + [dma((4,)), dma((4,))],
-    )(*results)
     return tuple(result[None] for result in results)
 
 

time: 103 us -> 105 us (1.019)
  local copies, waits for them, and re-layouts: 0 us -> 3.27 us
    unnamed x0 -> x4, local copies, waits for them, and re-layouts: none -> 3.27 us
    pallas_call x1 -> x0, Pallas kernels: 2.62 us -> none  [shards(): pl.pallas_call(pass_kernel, out_shape=(wide_one, wide_two, wide_one, wide...]
    pallas_call x1, Pallas kernels: 99.8 us -> 101 us  [shards(): pl.pallas_call(functools.partial(round_kernel, n_row, n_col, cap, kept),...]
where the time goes in v5:
time: 105 us
  Pallas kernels  101 us (96%)
  local copies, waits for them, and re-layouts  3.27 us (3%)
    pallas_call x1, Pallas kernels, shards(): pl.pallas_call(functools.partial(round_kernel, n_row, n_col, cap, kept),...  101 us
    unnamed x4, local copies, waits for them, and re-layouts  3.27 us

profile of v5, /device:TPU:0, one launch (start us, length us, event | category | flops | bytes accessed | tf_op | source)
XLA Modules:
  0.0 105.0 jit_solution(145215787542170344)
XLA Ops:
  0.6 101.0 %shard_map.93 = (f32[112,896]{1,0:T(8,128)S(1)}, f32[224,896]{1,0:T(8,128)S(1)}, f32[112,896]{1,0:T(8,128)S(1)}, f32[224,896]{1,0:T(8,128)S(1)}) custom-call(s32[1,128]{1,0:T(1,128)} %bitcast.17, bf16[128,4,896]{2,1,0:T(4,128)(2,1)} %docs_hbm.1, f32[112,896]{1,0:T(8,128)} %bitcast.15, f32[224,896]{1,0:T(8,128)} %bitcast.13, f32[112,896]{1,0:T(8,128)} %bitcast.16, ...), custom_call_target="tpu_custom_call" | custom-call | tf_op jit(solution)/shard_map/pallas_call | solution.py:624
  101.7 0.8 copy.14
  102.4 0.9 copy.15
  103.3 0.7 copy.16
  104.1 0.9 copy.17

commit v6 on v5

--- a/solution.py
+++ b/solution.py
@@ -207,8 +207,15 @@
             ),
         )
 
-    def apart(k, flip):
-        return (k + flip * (chips - 2 * k)) % chips
+    def apart(k, other_order):
+        near = k + inner * (other_order - k)
+        return (near + upper * (chips - 2 * near)) % chips
+
+    def last_first(k):
+        return (k + chips - 3) % (chips - 1) + 1
+
+    def backwards(k):
+        return (2 * chips - 1 - k) % (chips - 1) + 1
 
     def send_docs(first, last):
         def body(u, carry):
@@ -222,11 +229,8 @@
     counts[0] = cnt_ref[me]
     send_docs(1, group)
 
-    for k in range(1, chips - 1):
-        at = apart(k, upper) * group
-        send_docs(at, at + group)
-    at = apart(chips - 1, upper) * group
-    send_docs(at, at + half_group)
+    at = apart(1, last_first(1)) * group
+    send_docs(at, at + group)
 
     @pl.when(place == entry)
     def _():
@@ -237,7 +241,9 @@
             for j in range(1, side):
                 relay(source, sibling(j)).start()
 
-    send_docs(at + half_group, at + group)
+    for k in range(2, chips):
+        at = apart(k, last_first(k)) * group
+        send_docs(at, at + group)
     for j in range(1, side):
         relay(sibling(j), place).wait_recv()
         across(2 * sibling(j) + core).start()
@@ -254,8 +260,10 @@
         two_wait(k).wait_recv()
 
     def place_of(k):
-        flip = upper * inner + (1 - upper) * outer
-        return apart(k // 2, flip) * group + k % 2 * half_group
+        q = k // 2
+        near = (inner * backwards(q) + outer * last_first(q)) * ((q + chips - 1) // chips)
+        far_off = (near + upper * (chips - 2 * near)) % chips
+        return far_off * group + k % 2 * half_group
 
     def arrive(first, last):
         def body(u, carry):

time: 105 us -> 101 us (0.962)
  Pallas kernels: 101 us -> 97.3 us
    pallas_call x1, Pallas kernels: 101 us -> 97.3 us  [shards(): pl.pallas_call(functools.partial(round_kernel, n_row, n_col, cap, kept),...]
where the time goes in v6:
time: 101 us
  Pallas kernels  97.3 us (96%)
  local copies, waits for them, and re-layouts  3.27 us (3%)
    pallas_call x1, Pallas kernels, shards(): pl.pallas_call(functools.partial(round_kernel, n_row, n_col, cap, kept),...  97.3 us
    unnamed x4, local copies, waits for them, and re-layouts  3.27 us

profile of v6, /device:TPU:0, one launch (start us, length us, event | category | flops | bytes accessed | tf_op | source)
XLA Modules:
  0.0 101.3 jit_solution(15701423929242867245)
XLA Ops:
  0.6 97.3 %shard_map.93 = (f32[112,896]{1,0:T(8,128)S(1)}, f32[224,896]{1,0:T(8,128)S(1)}, f32[112,896]{1,0:T(8,128)S(1)}, f32[224,896]{1,0:T(8,128)S(1)}) custom-call(s32[1,128]{1,0:T(1,128)} %bitcast.17, bf16[128,4,896]{2,1,0:T(4,128)(2,1)} %docs_hbm.1, f32[112,896]{1,0:T(8,128)} %bitcast.15, f32[224,896]{1,0:T(8,128)} %bitcast.13, f32[112,896]{1,0:T(8,128)} %bitcast.16, ...), custom_call_target="tpu_custom_call" | custom-call | tf_op jit(solution)/shard_map/pallas_call | solution.py:632
  98.0 0.8 copy.14
  98.7 0.9 copy.15
  99.6 0.7 copy.16
  100.4 0.9 copy.17

commit v7 on v6

--- a/solution.py
+++ b/solution.py
@@ -207,15 +207,12 @@
             ),
         )
 
-    def apart(k, other_order):
-        near = k + inner * (other_order - k)
+    def apart(k):
+        near = outer * (k * 2 % chips + k // side) + inner * last_first(k)
         return (near + upper * (chips - 2 * near)) % chips
 
     def last_first(k):
         return (k + chips - 3) % (chips - 1) + 1
-
-    def backwards(k):
-        return (2 * chips - 1 - k) % (chips - 1) + 1
 
     def send_docs(first, last):
         def body(u, carry):
@@ -229,7 +226,7 @@
     counts[0] = cnt_ref[me]
     send_docs(1, group)
 
-    at = apart(1, last_first(1)) * group
+    at = apart(1) * group
     send_docs(at, at + group)
 
     @pl.when(place == entry)
@@ -242,7 +239,7 @@
                 relay(source, sibling(j)).start()
 
     for k in range(2, chips):
-        at = apart(k, last_first(k)) * group
+        at = apart(k) * group
         send_docs(at, at + group)
     for j in range(1, side):
         relay(sibling(j), place).wait_recv()
@@ -261,7 +258,7 @@
 
     def place_of(k):
         q = k // 2
-        near = (inner * backwards(q) + outer * last_first(q)) * ((q + chips - 1) // chips)
+        near = last_first(q) * ((q + chips - 1) // chips)
         far_off = (near + upper * (chips - 2 * near)) % chips
         return far_off * group + k % 2 * half_group
 
@@ -575,6 +572,14 @@
     def _():
         sone_copy(far(side - 1)).wait_send()
         pre_copy(place).wait_send()
+
+
+def store_kernel(*refs):
+    copies = [pltpu.make_async_copy(refs[i], refs[4 + i], refs[8].at[i]) for i in range(4)]
+    for copy in copies:
+        copy.start()
+    for copy in copies:
+        copy.wait()
 
 
 def shards(docs, routes, level_one, level_two, moment_one, moment_two):
@@ -641,6 +646,13 @@
     )(
         routes.reshape(1, count), docs, level_one[0], level_two[0], moment_one[0], moment_two[0]
     )
+    results = pl.pallas_call(
+        store_kernel,
+        out_shape=tuple(jax.ShapeDtypeStruct(result.shape, f32) for result in results),
+        in_specs=[hbm] * 4,
+        out_specs=(pl.BlockSpec(memory_space=pltpu.HBM),) * 4,
+        scratch_shapes=[dma((4,))],
+    )(*(pltpu.with_memory_space_constraint(result, pltpu.VMEM) for result in results))
     return tuple(result[None] for result in results)
 
 

time: 101 us -> 99.5 us (0.985)
  local copies, waits for them, and re-layouts: 3.27 us -> 0 us
    unnamed x4 -> x0, local copies, waits for them, and re-layouts: 3.27 us -> none
    pallas_call x0 -> x1, Pallas kernels: none -> 1.45 us  [shards(): pl.pallas_call(store_kernel, out_shape=tuple((jax.ShapeDtypeStruct(result...]
where the time goes in v7:
time: 99.5 us; the launch traced here: 99.1 us
  Pallas kernels  98.3 us (99%)
    pallas_call x1, Pallas kernels, shards(): pl.pallas_call(functools.partial(round_kernel, n_row, n_col, cap, kept),...  96.9 us

profile of v7, /device:TPU:0, one launch (start us, length us, event | category | flops | bytes accessed | tf_op | source)
XLA Modules:
  0.0 99.1 jit_solution(17979388600063026537)
XLA Ops:
  0.6 96.9 %shard_map.93 = (f32[112,896]{1,0:T(8,128)S(1)}, f32[224,896]{1,0:T(8,128)S(1)}, f32[112,896]{1,0:T(8,128)S(1)}, f32[224,896]{1,0:T(8,128)S(1)}) custom-call(s32[1,128]{1,0:T(1,128)} %bitcast.13, bf16[128,4,896]{2,1,0:T(4,128)(2,1)} %docs_hbm.1, f32[112,896]{1,0:T(8,128)} %bitcast.11, f32[224,896]{1,0:T(8,128)} %bitcast.9, f32[112,896]{1,0:T(8,128)} %bitcast.12, ...), custom_call_target="tpu_custom_call" | custom-call | tf_op jit(solution)/shard_map/pallas_call | solution.py:637
  97.5 1.5 %shard_map.94 = (f32[112,896]{1,0:T(8,128)}, f32[224,896]{1,0:T(8,128)}, f32[112,896]{1,0:T(8,128)}, f32[224,896]{1,0:T(8,128)}) custom-call(f32[112,896]{1,0:T(8,128)S(1)} %get-tuple-element.12.refs_0_, f32[224,896]{1,0:T(8,128)S(1)} %get-tuple-element.13.refs_1_, f32[112,896]{1,0:T(8,128)S(1)} %get-tuple-element.14.refs_2_, ...), custom_call_target="tpu_custom_call" | custom-call | tf_op jit(solution)/shard_map/pallas_call | solution.py:649

commit v8 on v7

--- a/solution.py
+++ b/solution.py
@@ -64,9 +64,7 @@
     rows = z.shape[0]
     per = rows // n
     group = 2 * n_row
-    half_group = group // 2
-    chunk = half_group * per
-    chunks = 2 * chips
+    chunk = group * per
     early = rows * (chips - 1) // chips // 256 * 256
     count = docs_v.shape[0]
     length = docs_v.shape[1]
@@ -257,10 +255,8 @@
         two_wait(k).wait_recv()
 
     def place_of(k):
-        q = k // 2
-        near = last_first(q) * ((q + chips - 1) // chips)
-        far_off = (near + upper * (chips - 2 * near)) % chips
-        return far_off * group + k % 2 * half_group
+        near = last_first(k) * ((k + chips - 1) // chips)
+        return (near + upper * (chips - 2 * near)) % chips * group
 
     def arrive(first, last):
         def body(u, carry):
@@ -271,7 +267,7 @@
         lax.fori_loop(first, last, body, 0)
 
     def unpack(k, at):
-        block = arrived[pl.ds(place_of(k), half_group)].astype(f32)
+        block = arrived[pl.ds(place_of(k), group)].astype(f32)
         if per == kept:
             first, last = block[:, :kept], block[:, lines - kept :]
         else:
@@ -337,7 +333,7 @@
     def two_rows(cols):
         return whole_two[...].reshape(width, width)[cols.start : cols.start + cols.size]
 
-    arrive(1, half_group)
+    arrive(1, group)
     low, high = pl.ds(0, early), pl.ds(early, rows - early)
 
     def first_turn(k, carry):
@@ -352,21 +348,21 @@
         errors(at, two_cols)
         slopes(at, two_rows, None)
 
-        @pl.when(k == chunks - 3)
+        @pl.when(k == chips - 2)
         def _():
             gram[low, low] = product(xb[low, :], xb[low, :], 1, 1).astype(bf16)
             for n0, nn in blocks:
                 cols = pl.ds(n0, nn)
                 dw[:, cols] = product(hb[low, :], eb[low, cols], 0, 0)
 
-        @pl.when(k < chunks - 1)
+        @pl.when(k < chips - 1)
         def _():
             first = place_of(k + 1)
-            arrive(first, first + half_group)
+            arrive(first, first + group)
 
         return carry
 
-    lax.fori_loop(0, chunks, first_turn, 0)
+    lax.fori_loop(0, chips, first_turn, 0)
     gram[high, :] = product(xb[high, :], xb[...], 1, 1).astype(bf16)
     gram[low, high] = product(xb[low, :], xb[high, :], 1, 1).astype(bf16)
 

time: 99.5 us -> 100 us (level)
  no operation moved by 1% of the time
where the time goes in v8:
time: 100 us; the launch traced here: 99.6 us
  Pallas kernels  98.8 us (99%)
    pallas_call x1, Pallas kernels, shards(): pl.pallas_call(functools.partial(round_kernel, n_row, n_col, cap, kept),...  97.4 us

profile of v8, /device:TPU:0, one launch (start us, length us, event | category | flops | bytes accessed | tf_op | source)
XLA Modules:
  0.0 99.6 jit_solution(5987131259613223133)
XLA Ops:
  0.6 97.4 %shard_map.93 = (f32[112,896]{1,0:T(8,128)S(1)}, f32[224,896]{1,0:T(8,128)S(1)}, f32[112,896]{1,0:T(8,128)S(1)}, f32[224,896]{1,0:T(8,128)S(1)}) custom-call(s32[1,128]{1,0:T(1,128)} %bitcast.13, bf16[128,4,896]{2,1,0:T(4,128)(2,1)} %docs_hbm.1, f32[112,896]{1,0:T(8,128)} %bitcast.11, f32[224,896]{1,0:T(8,128)} %bitcast.9, f32[112,896]{1,0:T(8,128)} %bitcast.12, ...), custom_call_target="tpu_custom_call" | custom-call | tf_op jit(solution)/shard_map/pallas_call | solution.py:633
  98.0 1.5 %shard_map.94 = (f32[112,896]{1,0:T(8,128)}, f32[224,896]{1,0:T(8,128)}, f32[112,896]{1,0:T(8,128)}, f32[224,896]{1,0:T(8,128)}) custom-call(f32[112,896]{1,0:T(8,128)S(1)} %get-tuple-element.12.refs_0_, f32[224,896]{1,0:T(8,128)S(1)} %get-tuple-element.13.refs_1_, f32[112,896]{1,0:T(8,128)S(1)} %get-tuple-element.14.refs_2_, ...), custom_call_target="tpu_custom_call" | custom-call | tf_op jit(solution)/shard_map/pallas_call | solution.py:645

commit v9 on v7

--- a/solution.py
+++ b/solution.py
@@ -94,8 +94,6 @@
     lax.fori_loop(1, n, greet, 0)
     loads[0].wait()
     whole_one[col] = new_one[...].astype(bf16)
-    loads[1].wait()
-    whole_two[row] = new_two[...].astype(bf16)
 
     pl.semaphore_wait(barrier, n - 1)
 
@@ -161,6 +159,8 @@
     for j in range(1, side):
         own_copy(sibling(j)).start()
     across(col).start()
+    loads[1].wait()
+    whole_two[row] = new_two[...].astype(bf16)
     for k in range(1, n_row):
         two_copy(k).start()
 
@@ -511,6 +511,25 @@
         moment[...] = following
         level[...] = level[...] - outer_rate * (share + momentum_decay * following)
 
+    def sent(u, carry):
+        for copy in pair_of(u):
+            copy.wait_send()
+        return carry
+
+    lax.fori_loop(1, n, sent, 0)
+    own_copy(other_entry).wait_send()
+    for j in range(1, side):
+        own_copy(sibling(j)).wait_send()
+
+    @pl.when(place == entry)
+    def _():
+        for i in range(side):
+            for j in range(1, side):
+                relay(beyond(i), sibling(j)).wait_send()
+
+    for q in range(chips):
+        across(2 * q + core).wait_send()
+
     share = two_out[row].astype(f32)
     for k in range(1, n_row):
         stwo_copy(k).wait_recv()
@@ -536,24 +555,7 @@
 
     finish(total[...] / n_col, new_one, next_one)
 
-    def sent(u, carry):
-        for copy in pair_of(u):
-            copy.wait_send()
-        return carry
-
-    lax.fori_loop(1, n, sent, 0)
-    own_copy(other_entry).wait_send()
-    for j in range(1, side):
-        own_copy(sibling(j)).wait_send()
-
-    @pl.when(place == entry)
-    def _():
-        for i in range(side):
-            for j in range(1, side):
-                relay(beyond(i), sibling(j)).wait_send()
-
     for q in range(chips):
-        across(2 * q + core).wait_send()
         spair_copy(q).wait_send()
     for k in range(1, n_row):
         two_copy(k).wait_send()

time: 99.5 us -> 99.1 us (level)
  no operation moved by 1% of the time
where the time goes in v9:
time: 99.1 us; the launch traced here: 98.7 us
  Pallas kernels  97.9 us (99%)
    pallas_call x1, Pallas kernels, shards(): pl.pallas_call(functools.partial(round_kernel, n_row, n_col, cap, kept),...  96.5 us

profile of v9, /device:TPU:0, one launch (start us, length us, event | category | flops | bytes accessed | tf_op | source)
XLA Modules:
  0.0 98.7 jit_solution(13562582749477722518)
XLA Ops:
  0.6 96.5 %shard_map.93 = (f32[112,896]{1,0:T(8,128)S(1)}, f32[224,896]{1,0:T(8,128)S(1)}, f32[112,896]{1,0:T(8,128)S(1)}, f32[224,896]{1,0:T(8,128)S(1)}) custom-call(s32[1,128]{1,0:T(1,128)} %bitcast.13, bf16[128,4,896]{2,1,0:T(4,128)(2,1)} %docs_hbm.1, f32[112,896]{1,0:T(8,128)} %bitcast.11, f32[224,896]{1,0:T(8,128)} %bitcast.9, f32[112,896]{1,0:T(8,128)} %bitcast.12, ...), custom_call_target="tpu_custom_call" | custom-call | tf_op jit(solution)/shard_map/pallas_call | solution.py:639
  97.1 1.5 %shard_map.94 = (f32[112,896]{1,0:T(8,128)}, f32[224,896]{1,0:T(8,128)}, f32[112,896]{1,0:T(8,128)}, f32[224,896]{1,0:T(8,128)}) custom-call(f32[112,896]{1,0:T(8,128)S(1)} %get-tuple-element.12.refs_0_, f32[224,896]{1,0:T(8,128)S(1)} %get-tuple-element.13.refs_1_, f32[112,896]{1,0:T(8,128)S(1)} %get-tuple-element.14.refs_2_, ...), custom_call_target="tpu_custom_call" | custom-call | tf_op jit(solution)/shard_map/pallas_call | solution.py:651

commit v10 on v9

--- a/solution.py
+++ b/solution.py
@@ -368,7 +368,7 @@
 
     lax.fori_loop(0, chunks, first_turn, 0)
     gram[high, :] = product(xb[high, :], xb[...], 1, 1).astype(bf16)
-    gram[low, high] = product(xb[low, :], xb[high, :], 1, 1).astype(bf16)
+    gram[low, high] = gram[high, low].T
 
     filled = jnp.sum(counts[...].reshape(n, 128), axis=0, keepdims=True)[:, :1]
     rate = inner_rate * scale / (filled * (length - 1))

time: 99.1 us -> 98.6 us (level)
  no operation moved by 1% of the time
where the time goes in v10:
time: 98.6 us; the launch traced here: 98.4 us
  Pallas kernels  97.8 us (99%)
    pallas_call x1, Pallas kernels, shards(): pl.pallas_call(functools.partial(round_kernel, n_row, n_col, cap, kept),...  96.3 us

profile of v10, /device:TPU:0, one launch (start us, length us, event | category | flops | bytes accessed | tf_op | source)
XLA Modules:
  0.0 98.4 jit_solution(5026003026033874126)
XLA Ops:
  0.6 96.3 %shard_map.93 = (f32[112,896]{1,0:T(8,128)S(1)}, f32[224,896]{1,0:T(8,128)S(1)}, f32[112,896]{1,0:T(8,128)S(1)}, f32[224,896]{1,0:T(8,128)S(1)}) custom-call(s32[1,128]{1,0:T(1,128)} %bitcast.13, bf16[128,4,896]{2,1,0:T(4,128)(2,1)} %docs_hbm.1, f32[112,896]{1,0:T(8,128)} %bitcast.11, f32[224,896]{1,0:T(8,128)} %bitcast.9, f32[112,896]{1,0:T(8,128)} %bitcast.12, ...), custom_call_target="tpu_custom_call" | custom-call | tf_op jit(solution)/shard_map/pallas_call | solution.py:639
  96.9 1.5 %shard_map.94 = (f32[112,896]{1,0:T(8,128)}, f32[224,896]{1,0:T(8,128)}, f32[112,896]{1,0:T(8,128)}, f32[224,896]{1,0:T(8,128)}) custom-call(f32[112,896]{1,0:T(8,128)S(1)} %get-tuple-element.12.refs_0_, f32[224,896]{1,0:T(8,128)S(1)} %get-tuple-element.13.refs_1_, f32[112,896]{1,0:T(8,128)S(1)} %get-tuple-element.14.refs_2_, ...), custom_call_target="tpu_custom_call" | custom-call | tf_op jit(solution)/shard_map/pallas_call | solution.py:651
